TPU v7x, 512 devices: a whole 4x8x8 slice. The times are simulated.
512 devices in a mesh: req: 16 (over y, core), seq: 32 (over z, x).
Axes of the slice: x: 4, y: 8, z: 8, core: 2. Of those that a mesh axis runs over, the one named last changes fastest.
Arguments:
- latent_cache: bfloat16 [16, 16384, 576], P('req', 'seq'), may hold values from -16 to 16
- queries: bfloat16 [16, 3, 128, 576], P('req', None, 'seq'), may hold values from -16 to 16
- chosen: int32 [16, 3, 32], P('req'), may hold values from 0 to 255, as said below
- position: int32 [16], P('req'), may hold values from 16321 to 16384
- w_value: bfloat16 [128, 512, 128], P('seq'), may hold values from -1.5 to 1.5
- w_out: bfloat16 [16384, 7168], P('seq', 'req'), may hold values from -0.09375 to 0.09375
Outputs:
- mixed_out: bfloat16 [7168, 48], P(('req', 'seq'))
Inputs may be any that keep to these rules, and one draw needn't show every extreme that they name: `chosen`: block b holds positions b * 64 to b * 64 + 63, which lie on shard b // 8 of seq. A query's 32 numbers are distinct; at most 8 of them lie on one shard and exactly 8 on some shard, for every query; every query names the last block; its blocks on the other shards are spread as evenly as possible over those shards.
All inputs are finite; a program needn't handle non-finite values.
Results may differ from a plain program's by a relative error of at most 0.013.
Values may be sent and summed in bfloat16 or wider, within the bound.
No kernel may reach another device: no remote copies, remote signals or barrier semaphores. Data moves between devices by JAX's collectives and lax.ppermute only.
A program may use at most 128 MiB of HBM per device.

v0:
```python
import math

import jax
import jax.numpy as jnp
from jax import lax
from jax.sharding import PartitionSpec as P

LATENT = 512
BLOCK = 64
MAXB = 8


score_scale = 1.0 / math.sqrt(192.0)
very_low = -1e30


def sent_to_all(value, axis):
    size = lax.axis_size(axis)
    return lax.all_to_all(
        jnp.broadcast_to(value[None], (size, *value.shape)), axis, 0, 0, tiled=True
    )


def in_order(parts, dim):
    parts = jnp.moveaxis(parts, 0, dim)
    dims = parts.shape
    return parts.reshape(*dims[:dim], dims[dim] * dims[dim + 1], *dims[dim + 2 :])


def gathered_copies(value, axis, dim):
    parts = sent_to_all(value, axis)
    return in_order(parts, dim)


def of_everyone(value, axis):
    return sent_to_all(value, axis).max(axis=0)


def in_blocks(value, dim, size):
    before, after = (value.shape[:dim], value.shape[dim + 1 :])
    return jnp.moveaxis(value.reshape(*before, size, -1, *after), dim, 0)


def summed_on_arrival(value, axis, dim):
    size = lax.axis_size(axis)
    parts = lax.all_to_all(in_blocks(value, dim, size), axis, 0, 0, tiled=True)
    return jnp.sum(parts, axis=0)


def sent_together(arrays, axis, dim, along):
    widths = [math.prod(a.shape[along:]) for a in arrays]
    both = jnp.concatenate(
        [a.reshape(*a.shape[:along], w) for a, w in zip(arrays, widths)], axis=along
    )
    out = summed_on_arrival(both, axis, dim)
    parts = jnp.split(out, [sum(widths[:k]) for k in range(1, len(widths))], axis=along)
    return tuple((b.reshape(*out.shape[:along], *a.shape[along:]) for a, b in zip(arrays, parts)))


def local_blocks(chosen_rows, shard_index, per_shard):
    owned_here = (chosen_rows // per_shard == shard_index).astype(jnp.int32)
    ranked = jnp.cumsum(owned_here, axis=1) - 1
    target = jnp.arange(MAXB, dtype=jnp.int32)
    matched = (owned_here[:, :, None] == 1) & (ranked[:, :, None] == target[None, None, :])
    offset = jnp.sum(jnp.where(matched, (chosen_rows % per_shard)[:, :, None], 0), axis=1)
    return (offset, jnp.any(matched, axis=1))


def body(latent_cache, queries, chosen, position, w_value, w_out):
    req_dev, cache_len, key_width = latent_cache.shape
    step_count = queries.shape[1]
    query_count = req_dev * step_count
    per_shard = cache_len // BLOCK
    shard_index = lax.axis_index("seq")
    all_heads = gathered_copies(queries, "seq", 2)
    query_rows = all_heads.reshape(query_count, all_heads.shape[2], key_width)
    offset, filled = local_blocks(
        chosen.reshape(query_count, chosen.shape[2]), shard_index, per_shard
    )
    request_of = jnp.arange(query_count, dtype=jnp.int32) // step_count
    inside = jnp.arange(BLOCK, dtype=jnp.int32)
    local_row = offset[:, :, None] * BLOCK + inside[None, None, :]
    flat_rows = (request_of[:, None, None] * cache_len + local_row).reshape(query_count, -1)
    gathered = jnp.take(latent_cache.reshape(req_dev * cache_len, key_width), flat_rows, axis=0)
    position_limit = jnp.broadcast_to(position[:, None], (req_dev, step_count)).reshape(-1)
    usable = filled[:, :, None] & (
        shard_index * cache_len + local_row < position_limit[:, None, None]
    )
    usable = usable.reshape(query_count, -1)
    scores = (
        jnp.einsum("qhk,qnk->qhn", query_rows, gathered, preferred_element_type=jnp.float32)
        * score_scale
    )
    scores = jnp.where(usable[:, None, :], scores, very_low)
    row_peak = jnp.max(scores, axis=2)
    raw_weights = jnp.where(usable[:, None, :], jnp.exp(scores - row_peak[:, :, None]), 0.0)
    row_total = jnp.sum(raw_weights, axis=2)
    latent_part = lax.slice_in_dim(gathered, 0, LATENT, axis=2)
    weighted = jnp.einsum(
        "qhn,qnl->qhl",
        raw_weights.astype(jnp.bfloat16),
        latent_part,
        preferred_element_type=jnp.float32,
    )
    heads_dev = w_value.shape[0]
    peak_all = of_everyone(row_peak, "seq")
    factor = jnp.exp(row_peak - peak_all)
    weighted_mine, total_mine = sent_together(
        (weighted * factor[:, :, None], row_total * factor), "seq", 1, 2
    )
    latent_out = (weighted_mine / total_mine[:, :, None]).astype(jnp.bfloat16)
    head_out = jnp.einsum(
        "qhl,hlv->qhv", latent_out, w_value, preferred_element_type=jnp.float32
    ).astype(jnp.bfloat16)
    head_out = head_out.reshape(req_dev, step_count, heads_dev * w_value.shape[2])
    every_request = gathered_copies(head_out, "req", 0)
    flat_heads = every_request.reshape(-1, every_request.shape[2])
    mixed_out = summed_on_arrival(
        lax.dot_general(
            w_out, flat_heads, (((0,), (1,)), ((), ())), preferred_element_type=jnp.float32
        ),
        "seq",
        0,
    )
    return mixed_out.astype(jnp.bfloat16)


def solution(mesh):
    return jax.shard_map(
        body,
        mesh=mesh,
        in_specs=(
            P("req", "seq", None),
            P("req", None, "seq", None),
            P("req", None, None),
            P("req"),
            P("seq", None, None),
            P("seq", "req"),
        ),
        out_specs=P(("req", "seq"), None),
        check_vma=False,
    )
```

profile of v0, /device:TPU:1, one launch (start us, length us, event | category | flops | bytes accessed | tf_op | source)
XLA Modules:
  0.0 117.1 jit_solution(15113420067235416243)
XLA Ops:
  0.0 0.0 copy-start
  0.0 1.7 %broadcast_in_dim.87 = bf16[32,1,3,4,576]{4,3,2,1,0:T(4,128)(2,1)} broadcast(bf16[3,4,576]{2,1,0:T(4,128)(2,1)} %bitcast.50), dimensions={2,3,4} | broadcast | bytes 456192 | tf_op jit(solution)/shard_map/broadcast_in_dim | solution.py:20
  1.7 13.8 %all-to-all-start = ((bf16[32,1,3,4,576]{4,3,2,1,0:T(4,128)(2,1)}), bf16[32,1,3,4,576]{4,3,2,1,0:T(4,128)(2,1)}, u32[]{:S(2)}, u32[]{:S(2)}) async-start(bf16[32,1,3,4,576]{4,3,2,1,0:T(4,128)(2,1)} %broadcast_in_dim.87), calls=%async_computation | async-start | bytes 983040 | tf_op jit(solution)/shard_map/all_to_all | solution.py:19
  15.6 0.7 broadcast_compare_fusion.1
  16.3 0.2 reduce_window_sum.11
  16.5 0.7 add_select_fusion
  17.2 0.1 fusion.17
  17.3 0.2 select_reduce_fusion
  17.5 0.1 add.127
  17.5 0.1 add.128
  17.6 0.1 add.139
  17.7 0.1 and.76
  17.8 0.1 and.77
  17.9 0.1 add.130
  18.6 0.1 compare_select_fusion
  18.7 0.3 copy.50
  19.0 5.0 %gather_fusion = bf16[1536,576]{1,0:T(8,128)(2,1)S(1)} fusion(bf16[512,576]{1,0:T(8,128)(2,1)S(1)} %bitcast.48, s32[2048]{0:T(1024)S(1)} %pad_clamp_fusion), kind=kCustom, calls=%fused_computation | custom fusion | bytes 3545088 | tf_op jit(solution)/shard_map/jit(_take)/gather | solution.py:84
  24.0 0.1 fusion.18
  24.1 1.6 %broadcast_select_fusion = bf16[3,512,576]{2,1,0:T(8,128)(2,1)} fusion(bf16[3,512,576]{2,1,0:T(8,128)(2,1)S(1)} %bitcast.49, pred[3,512]{1,0:T(4,128)(4,1)S(1)} %get-tuple-element.10), kind=kLoop, calls=%fused_computation.1 | loop fusion | flops 884736 | bytes 3540480 | tf_op jit(solution)/shard_map/jit(_take)/select_n | solution.py:84
  25.7 5.2 %all-to-all-done = bf16[32,1,3,4,576]{4,3,2,1,0:T(4,128)(2,1)} async-done(((bf16[32,1,3,4,576]{4,3,2,1,0:T(4,128)(2,1)}), bf16[32,1,3,4,576]{4,3,2,1,0:T(4,128)(2,1)}, u32[]{:S(2)}, u32[]{:S(2)}) %all-to-all-start) | async-done | bytes 442400 | tf_op jit(solution)/shard_map/all_to_all | solution.py:19
  30.9 1.2 %copy.51 = bf16[1,3,32,4,576]{4,3,2,1,0:T(4,128)(2,1)S(1)} copy(bf16[1,3,32,4,576]{4,3,1,0,2:T(4,128)(2,1)} %bitcast.4) | data formatting | bytes 884736 | tf_op jit(solution)/shard_map/transpose | solution.py:25
  32.1 1.1 reshape_reshape.6
  33.2 0.0 copy-done.1
  33.2 1.7 %fusion.27 = (f32[3,128]{1,0:T(4,128)S(1)}, f32[3,128,512]{1,2,0:T(8,128)S(1)}) fusion(bf16[3,512,576]{2,1,0:T(8,128)(2,1)S(1)} %copy-done.1, bf16[3,128,576]{2,1,0:T(8,128)(2,1)} %reshape_reshape.6, pred[3,512]{1,0:T(4,128)(4,1)S(1)} %get-tuple-element.9), kind=kOutput, calls=%fused_computation.54 | convolution fusion | flops 227081856 | bytes 3001344 | tf_op jit(solution)/shard_map/qhk,qnk->qhn/dot_general | solution.py:91
  34.9 0.6 broadcast_in_dim.90
  35.5 5.5 %all-to-all-start.1 = ((f32[32,3,128]{2,1,0:T(4,128)}), f32[32,3,128]{2,1,0:T(4,128)S(1)}, u32[]{:S(2)}, u32[]{:S(2)}) async-start(f32[32,3,128]{2,1,0:T(4,128)} %broadcast_in_dim.90), calls=%async_computation.1 | async-start | bytes 131072 | tf_op jit(solution)/shard_map/all_to_all | solution.py:19
  41.0 0.3 fusion.8
  41.3 8.5 %all-to-all-done.1 = f32[32,3,128]{2,1,0:T(4,128)S(1)} async-done(((f32[32,3,128]{2,1,0:T(4,128)}), f32[32,3,128]{2,1,0:T(4,128)S(1)}, u32[]{:S(2)}, u32[]{:S(2)}) %all-to-all-start.1) | async-done | bytes 49184 | tf_op jit(solution)/shard_map/all_to_all | solution.py:19
  49.9 1.6 %fusion.2 = f32[3,128,512]{2,1,0:T(8,128)} fusion(bf16[3,512,576]{2,1,0:T(8,128)(2,1)S(1)} %copy-done.1, f32[3,128,512]{1,2,0:T(8,128)S(1)} %get-tuple-element.12, f32[3,128]{1,0:T(4,128)S(1)} %get-tuple-element.6, f32[3,128]{1,0:T(4,128)S(1)} %get-tuple-element.11, pred[3,512]{1,0:T(4,128)(4,1)S(1)} %get-tuple-element.9), kind=kOutput, calls=%fused_computation.4 | convolution fusion | flops 202113024 | bytes 3151872 | tf_op jit(solution)/shard_map/qhn,qnl->qhl/dot_general | solution.py:99
  51.5 1.4 %concatenate.6 = f32[3,32,4,512]{3,2,1,0:T(4,128)S(1)} reshape(f32[3,128,512]{2,1,0:T(8,128)} %fusion.2) | data formatting | bytes 1572864 | tf_op jit(solution)/shard_map/concatenate | solution.py:52
  52.9 0.1 mul.58
  53.0 0.7 copy.57
  53.7 0.2 maximum_bitcast_fusion
  53.9 0.0 copy-start.3
  53.9 27.0 %all_to_all.25 = f32[32,3,4,513]{3,2,1,0:T(4,128)S(1)} all-to-all(f32[32,3,4,513]{3,2,1,0:T(4,128)S(1)} %maximum_bitcast_fusion), channel_id=1, replica_groups=mesh['req'=16,'seq'=32] {'seq'}, dimensions={0} | all-to-all | bytes 1575936 | tf_op jit(solution)/shard_map/all_to_all | solution.py:46
  80.9 0.2 reduce_sum.38
  81.1 0.1 slice_reduce_fusion
  81.2 0.1 fusion.14
  81.3 0.2 fusion.7
  81.5 19.1 %all_to_all.26 = bf16[16,1,3,512]{3,2,1,0:T(4,128)(2,1)S(1)} all-to-all(bf16[16,1,3,512]{3,2,1,0:T(4,128)(2,1)S(1)} %broadcast_in_dim.92), channel_id=1, replica_groups=mesh['req'=16,'seq'=32] {'req'}, dimensions={0} | all-to-all | bytes 98304 | tf_op jit(solution)/shard_map/all_to_all | solution.py:19
  100.6 0.2 convolution_bitcast_fusion
  100.9 0.1 copy.60
  101.1 0.2 reshape.307
  101.3 13.6 %all_to_all.27 = f32[32,1,672]{2,1,0:T(1,128)S(1)} all-to-all(f32[32,1,672]{2,1,0:T(1,128)S(1)} %reshape.307), channel_id=1, replica_groups=mesh['req'=16,'seq'=32] {'seq'}, dimensions={0} | all-to-all | bytes 172032 | tf_op jit(solution)/shard_map/all_to_all | solution.py:46
  114.9 0.5 broadcast.272
  115.4 0.9 reduce.2
  116.3 0.1 reshape.308
  116.5 0.6 reduce_sum.39
  (15 shorter events, 0.2 us)
Async XLA Ops:
  0.0 81.3 %copy-start = (bf16[4,512,128]{2,1,0:T(8,128)(2,1)S(1)}, bf16[4,512,128]{2,1,0:T(8,128)(2,1)}, u32[]{:S(2)}) copy-start(bf16[4,512,128]{2,1,0:T(8,128)(2,1)} %param.10) | copy-start | bytes 1572868
  0.0 18.7 %copy-start.2 = (bf16[1,512,576]{1,2,0:T(8,128)(2,1)S(1)}, bf16[1,512,576]{1,2,0:T(8,128)(2,1)}, u32[]{:S(2)}) copy-start(bf16[1,512,576]{1,2,0:T(8,128)(2,1)} %param.6) | copy-start | bytes 1769476
  1.7 29.2 %all-to-all-start = ((bf16[32,1,3,4,576]{4,3,2,1,0:T(4,128)(2,1)}), bf16[32,1,3,4,576]{4,3,2,1,0:T(4,128)(2,1)}, u32[]{:S(2)}, u32[]{:S(2)}) async-start(bf16[32,1,3,4,576]{4,3,2,1,0:T(4,128)(2,1)} %broadcast_in_dim.87), calls=%async_computation | async-start | bytes 983040 | tf_op jit(solution)/shard_map/all_to_all | solution.py:19
  25.7 7.5 %copy-start.1 = (bf16[3,512,576]{2,1,0:T(8,128)(2,1)S(1)}, bf16[3,512,576]{2,1,0:T(8,128)(2,1)}, u32[]{:S(2)}) copy-start(bf16[3,512,576]{2,1,0:T(8,128)(2,1)} %broadcast_select_fusion) | copy-start | bytes 5308420
  35.5 14.3 %all-to-all-start.1 = ((f32[32,3,128]{2,1,0:T(4,128)}), f32[32,3,128]{2,1,0:T(4,128)S(1)}, u32[]{:S(2)}, u32[]{:S(2)}) async-start(f32[32,3,128]{2,1,0:T(4,128)} %broadcast_in_dim.90), calls=%async_computation.1 | async-start | bytes 131072 | tf_op jit(solution)/shard_map/all_to_all | solution.py:19
  53.9 46.7 %copy-start.3 = (bf16[512,448]{0,1:T(8,128)(2,1)S(1)}, bf16[512,448]{0,1:T(8,128)(2,1)}, u32[]{:S(2)}) copy-start(bf16[512,448]{0,1:T(8,128)(2,1)} %param.11) | copy-start | bytes 1376260
where the time goes:
time: 118 us; the launch traced here: 117 us
  blocking collectives  59.7 us (51%)
  starting transfers between devices  19.3 us (16%)
  local copies, waits for them, and re-layouts  13.7 us (12%)
  waiting for transfers between devices  13.7 us (12%)
  other arithmetic  6 us (5%)
  matrix products  3.72 us (3%)
    all_to_all x2, blocking collectives, summed_on_arrival(): parts = lax.all_to_all(in_blocks(value, dim, size), axis, 0, 0, tiled=True)  40.6 us
    all_to_all x2, starting transfers between devices, sent_to_all(): lax.all_to_all(jnp.broadcast_to(value[None], (size, *value.shape)), axis,...  19.3 us
    all_to_all x1, blocking collectives, sent_to_all(): lax.all_to_all(jnp.broadcast_to(value[None], (size, *value.shape)), axis,...  19.1 us
    all_to_all x2, waiting for transfers between devices, sent_to_all(): lax.all_to_all(jnp.broadcast_to(value[None], (size, *value.shape)), axis,...  13.7 us
    gather x1, local copies, waits for them, and re-layouts, body(): jnp.take(latent_cache.reshape(req_dev * cache_len, key_width), flat_rows,...  4.97 us
    broadcast_in_dim x3, local copies, waits for them, and re-layouts, sent_to_all(): jnp.broadcast_to(value[None], (size, *value.shape))  2.38 us
  transfers between devices with their start and end apart: 2, of which 2 were waited for; matrix products, arithmetic and copies ran while one was open for 8% of the time, Pallas kernels for 0%

commit v1 on v0

v1 whole, which is shorter than its diff:
```python
import functools
import math

import jax
import jax.numpy as jnp
from jax import lax
from jax.experimental import pallas as pl
from jax.experimental.pallas import tpu as pltpu
from jax.sharding import PartitionSpec as P

LATENT = 512
BLOCK = 64
LANES = 128

score_scale = 1.0 / math.sqrt(192.0)
very_low = -1e30
f32 = jnp.float32
bf16 = jnp.bfloat16


def pieces(value):
    high = value.astype(bf16).astype(f32)
    rest = value - high
    middle = rest.astype(bf16).astype(f32)
    return high, middle, rest - middle


def attend_kernel(usable_ref, query_ref, cache_ref, out_ref, rows_ref, sums_ref):
    shards, steps, heads_dev, _ = query_ref.shape
    heads = shards * heads_dev
    for t in range(steps):
        for s in range(shards):
            rows_ref[t, s * heads_dev : (s + 1) * heads_dev, :] = query_ref[s, t]
    keys = cache_ref[...]
    latent = keys[:, :LATENT]
    lane = lax.broadcasted_iota(jnp.int32, (heads, LANES), 1)
    for t in range(steps):
        usable = usable_ref[t : t + 1, :] > 0.0
        scores = (
            lax.dot_general(
                rows_ref[t], keys, (((1,), (1,)), ((), ())), preferred_element_type=f32
            )
            * score_scale
        )
        scores = jnp.where(usable, scores, very_low)
        peak = jnp.max(scores, axis=1, keepdims=True)
        raw = jnp.where(usable, jnp.exp(scores - peak), 0.0)
        total = jnp.sum(raw, axis=1, keepdims=True)
        weighted = jnp.dot(raw.astype(bf16), latent, preferred_element_type=f32)
        sums_ref[t, :, :LATENT] = weighted.astype(bf16)
        stats = jnp.zeros((heads, LANES), f32)
        for k, piece in enumerate(pieces(peak) + pieces(total)):
            stats = jnp.where(lane == k, piece, stats)
        sums_ref[t, :, LATENT:] = stats.astype(bf16)
    for t in range(steps):
        for s in range(shards):
            out_ref[s, t] = sums_ref[t, s * heads_dev : (s + 1) * heads_dev, :]


def merge_kernel(parts_ref, value_ref, out_ref):
    shards, steps, heads_dev, _ = parts_ref.shape
    rows = []
    for t in range(steps):
        stats = parts_ref[:, t, :, LATENT:].astype(f32)
        peak = stats[:, :, 0:1] + stats[:, :, 1:2] + stats[:, :, 2:3]
        total = stats[:, :, 3:4] + stats[:, :, 4:5] + stats[:, :, 5:6]
        factor = jnp.exp(peak - jnp.max(peak, axis=0, keepdims=True))
        parts = parts_ref[:, t, :, :LATENT].astype(f32)
        latent_out = jnp.sum(parts * factor, axis=0) / jnp.sum(total * factor, axis=0)
        rows.append(latent_out.astype(bf16))
    row = lax.broadcasted_iota(jnp.int32, (heads_dev, value_ref.shape[2]), 0)
    for t in range(steps):
        for h in range(heads_dev):
            product = jnp.dot(rows[t], value_ref[h], preferred_element_type=f32)
            mine = jnp.sum(jnp.where(row == h, product, 0.0), axis=0, keepdims=True)
            width = value_ref.shape[2]
            out_ref[t : t + 1, h * width : (h + 1) * width] = mine.astype(bf16)


def exchanged(value, axis):
    return lax.all_to_all(value, axis, 0, 0, tiled=True)


def body(latent_cache, queries, chosen, position, w_value, w_out):
    cache_len, key_width = latent_cache.shape[1:]
    _, steps, heads_dev, _ = queries.shape
    shards = lax.axis_size("seq")
    requests = lax.axis_size("req")
    shard_index = lax.axis_index("seq")

    query_all = exchanged(
        jnp.broadcast_to(queries, (shards, steps, heads_dev, key_width)), "seq"
    )
    blocks = shard_index * (cache_len // BLOCK) + jnp.arange(cache_len, dtype=jnp.int32) // BLOCK
    rows = shard_index * cache_len + jnp.arange(cache_len, dtype=jnp.int32)
    usable = jnp.any(chosen[0][:, :, None] == blocks, axis=1) & (rows < position[0])
    message = LATENT + LANES
    parts = pl.pallas_call(
        attend_kernel,
        out_shape=jax.ShapeDtypeStruct((shards, steps, heads_dev, message), bf16),
        scratch_shapes=[
            pltpu.VMEM((steps, shards * heads_dev, key_width), bf16),
            pltpu.VMEM((steps, shards * heads_dev, message), bf16),
        ],
        name="attend",
    )(usable.astype(f32), query_all, latent_cache.reshape(cache_len, key_width))
    parts = exchanged(parts, "seq")
    vdim = w_value.shape[2]
    head_out = pl.pallas_call(
        merge_kernel,
        out_shape=jax.ShapeDtypeStruct((steps, heads_dev * vdim), bf16),
        name="merge",
    )(parts, w_value)
    every_request = exchanged(
        jnp.broadcast_to(head_out[None], (requests, *head_out.shape)), "req"
    )
    flat_heads = every_request.reshape(requests * steps, heads_dev * vdim)
    partial = lax.dot_general(
        w_out, flat_heads, (((0,), (1,)), ((), ())), preferred_element_type=f32
    ).astype(bf16)
    mixed = exchanged(partial.reshape(shards, 1, -1), "seq")
    mixed = jnp.sum(mixed.astype(f32), axis=0).astype(bf16)
    return mixed.reshape(-1, requests * steps)


def solution(mesh):
    return jax.shard_map(
        body,
        mesh=mesh,
        in_specs=(
            P("req", "seq", None),
            P("req", None, "seq", None),
            P("req", None, None),
            P("req"),
            P("seq", None, None),
            P("seq", "req"),
        ),
        out_specs=P(("req", "seq"), None),
        check_vma=False,
    )
```

time: 118 us -> 93.6 us (0.79)
  blocking collectives: 59.7 us -> 51.2 us
  local copies, waits for them, and re-layouts: 13.7 us -> 6.75 us
  Pallas kernels: 0 us -> 6.21 us
  starting transfers between devices: 19.3 us -> 13.8 us
  other arithmetic: 6 us -> 1.75 us
  matrix products: 3.72 us -> 0.23 us
  waiting for transfers between devices: 13.7 us -> 12.2 us
    all_to_all x3, blocking collectives: 59.7 us -> 51.2 us  [exchanged(): return lax.all_to_all(value, axis, 0, 0, tiled=True)]
    pallas_call x0 -> x2, Pallas kernels: none -> 6.21 us  [the longest x1 3.68 us: body(): pl.pallas_call(attend_kernel, out_shape=jax.ShapeDtypeStruct((shards, ste...]
    all_to_all x2 -> x1, starting transfers between devices: 19.3 us -> 13.8 us  [exchanged(): return lax.all_to_all(value, axis, 0, 0, tiled=True)]
    gather x1 -> x0, local copies, waits for them, and re-layouts: 4.97 us -> none  [body(): jnp.take(latent_cache.reshape(req_dev * cache_len, key_width), flat_rows,...]
    dot_general x3 -> x0, matrix products: 3.48 us -> none  [the longest x1 1.72 us: body(): jnp.einsum('qhk,qnk->qhn', query_rows, gathered, preferred_element_type=j...]
    select_n x3 -> x0, other arithmetic: 2.39 us -> none  [the longest x2 1.7 us: body(): jnp.take(latent_cache.reshape(req_dev * cache_len, key_width), flat_rows,...]
    unnamed x11 -> x12, local copies, waits for them, and re-layouts: 0.68 us -> 2.8 us
    all_to_all x2 -> x1, waiting for transfers between devices: 13.7 us -> 12.2 us  [exchanged(): return lax.all_to_all(value, axis, 0, 0, tiled=True)]
  transfers between devices with their start and end apart: 2 -> 1, of which waited for: 2 -> 1; matrix products, arithmetic and copies ran while one was open for 8% -> 2% of each run, Pallas kernels for 0% -> 0%
where the time goes in v1:
time: 93.6 us; the launch traced here: 93 us
  blocking collectives  51.2 us (55%)
  starting transfers between devices  13.8 us (15%)
  waiting for transfers between devices  12.2 us (13%)
  local copies, waits for them, and re-layouts  6.75 us (7%)
  Pallas kernels  6.21 us (7%)
  other arithmetic  1.75 us (2%)
    all_to_all x3, blocking collectives, exchanged(): return lax.all_to_all(value, axis, 0, 0, tiled=True)  51.2 us
    all_to_all x1, starting transfers between devices, exchanged(): return lax.all_to_all(value, axis, 0, 0, tiled=True)  13.8 us
    all_to_all x1, waiting for transfers between devices, exchanged(): return lax.all_to_all(value, axis, 0, 0, tiled=True)  12.2 us
    pallas_call x1, Pallas kernels, body(): pl.pallas_call(attend_kernel, out_shape=jax.ShapeDtypeStruct((shards, ste...  3.68 us
    unnamed x12, local copies, waits for them, and re-layouts  2.8 us
    pallas_call x1, Pallas kernels, body(): pl.pallas_call(merge_kernel, out_shape=jax.ShapeDtypeStruct((steps, heads...  2.53 us
  transfers between devices with their start and end apart: 1, of which 1 were waited for; matrix products, arithmetic and copies ran while one was open for 2% of the time, Pallas kernels for 0%

profile of v1, /device:TPU:1, one launch (start us, length us, event | category | flops | bytes accessed | tf_op | source)
XLA Modules:
  0.0 93.0 jit_solution(13389316775415903422)
XLA Ops:
  0.0 0.0 copy-start
  0.0 1.7 %broadcast_in_dim.7 = bf16[32,3,4,576]{3,2,1,0:T(4,128)(2,1)} broadcast(bf16[3,4,576]{2,1,0:T(4,128)(2,1)} %bitcast.12), dimensions={1,2,3} | broadcast | bytes 456192 | tf_op jit(solution)/shard_map/broadcast_in_dim | solution.py:92
  1.7 0.0 copy-start.2
  1.7 13.8 %all-to-all-start = ((bf16[32,3,4,576]{3,2,1,0:T(4,128)(2,1)}), bf16[32,3,4,576]{3,2,1,0:T(4,128)(2,1)S(1)}, u32[]{:S(2)}, u32[]{:S(2)}) async-start(bf16[32,3,4,576]{3,2,1,0:T(4,128)(2,1)} %broadcast_in_dim.7), calls=%async_computation | async-start | bytes 983040 | tf_op jit(solution)/shard_map/all_to_all | solution.py:81
  15.5 0.0 copy-start.3
  15.5 0.7 copy-done.3
  16.9 0.0 copy-done.2
  16.9 1.1 %copy.13 = bf16[1,512,576]{2,1,0:T(8,128)(2,1)} copy(bf16[1,512,576]{1,2,0:T(8,128)(2,1)S(1)} %copy-done.2) | data formatting | bytes 1179648 | tf_op args[0]
  18.0 0.1 compare_reduce_fusion
  18.1 0.6 and_convert_fusion.usable_ref
  18.7 12.2 %all-to-all-done.query_ref = bf16[32,3,4,576]{3,2,1,0:T(4,128)(2,1)S(1)} async-done(((bf16[32,3,4,576]{3,2,1,0:T(4,128)(2,1)}), bf16[32,3,4,576]{3,2,1,0:T(4,128)(2,1)S(1)}, u32[]{:S(2)}, u32[]{:S(2)}) %all-to-all-start) | async-done | bytes 442400 | tf_op jit(solution)/shard_map/all_to_all | solution.py:81
  30.9 0.0 copy-start.1
  30.9 0.8 copy-done.1
  31.7 3.7 %attend.1 = bf16[32,3,4,640]{3,2,1,0:T(4,128)(2,1)} custom-call(f32[3,512]{1,0:T(4,128)} %and_convert_fusion.usable_ref, bf16[32,3,4,576]{3,2,1,0:T(4,128)(2,1)} %copy-done.1, bf16[512,576]{1,0:T(8,128)(2,1)} %bitcast.11), custom_call_target="tpu_custom_call" | custom-call | tf_op jit(solution)/shard_map/attend/pallas_call | solution.py:98
  35.4 20.3 %all_to_all.20.parts_ref = bf16[32,3,4,640]{3,2,1,0:T(4,128)(2,1)} all-to-all(bf16[32,3,4,640]{3,2,1,0:T(4,128)(2,1)} %attend.1), channel_id=1, replica_groups=mesh['req'=16,'seq'=32] {'seq'}, dimensions={0} | all-to-all | bytes 983040 | tf_op jit(solution)/shard_map/all_to_all | solution.py:81
  55.7 2.5 %merge.1 = bf16[3,512]{1,0:T(4,128)(2,1)} custom-call(bf16[32,3,4,640]{3,2,1,0:T(4,128)(2,1)} %all_to_all.20.parts_ref, bf16[4,512,128]{2,1,0:T(8,128)(2,1)} %value_ref.1), custom_call_target="tpu_custom_call" | custom-call | tf_op jit(solution)/shard_map/merge/pallas_call | solution.py:109
  58.2 0.7 broadcast_in_dim.8
  58.9 18.2 %all_to_all.21 = bf16[16,3,512]{2,1,0:T(4,128)(2,1)S(1)} all-to-all(bf16[16,3,512]{2,1,0:T(4,128)(2,1)S(1)} %broadcast_in_dim.8), channel_id=1, replica_groups=mesh['req'=16,'seq'=32] {'req'}, dimensions={0} | all-to-all | bytes 98304 | tf_op jit(solution)/shard_map/all_to_all | solution.py:81
  77.2 0.0 copy-done
  77.2 0.2 fusion
  77.4 0.1 copy.14
  77.6 0.2 reshape.39
  77.8 0.5 broadcast.42
  78.3 0.9 reduce.2
  79.2 0.1 reshape.40
  79.3 12.7 %all_to_all.22 = bf16[32,2,336]{2,1,0:T(2,128)(2,1)S(1)} all-to-all(bf16[32,2,336]{2,1,0:T(2,128)(2,1)S(1)} %reshape.40), channel_id=1, replica_groups=mesh['req'=16,'seq'=32] {'seq'}, dimensions={0} | all-to-all | bytes 86016 | tf_op jit(solution)/shard_map/all_to_all | solution.py:81
  92.1 0.1 reshape.41
  92.2 0.1 reduce_sum.12
  92.3 0.7 reshape.38
  (4 shorter events, 0.1 us)
Async XLA Ops:
  0.0 77.2 %copy-start = (bf16[512,448]{0,1:T(8,128)(2,1)S(1)}, bf16[512,448]{0,1:T(8,128)(2,1)}, u32[]{:S(2)}) copy-start(bf16[512,448]{0,1:T(8,128)(2,1)} %param.11) | copy-start | bytes 1376260
  1.7 15.2 %copy-start.2 = (bf16[1,512,576]{1,2,0:T(8,128)(2,1)S(1)}, bf16[1,512,576]{1,2,0:T(8,128)(2,1)}, u32[]{:S(2)}) copy-start(bf16[1,512,576]{1,2,0:T(8,128)(2,1)} %param.6) | copy-start | bytes 1769476
  1.7 29.2 %all-to-all-start = ((bf16[32,3,4,576]{3,2,1,0:T(4,128)(2,1)}), bf16[32,3,4,576]{3,2,1,0:T(4,128)(2,1)S(1)}, u32[]{:S(2)}, u32[]{:S(2)}) async-start(bf16[32,3,4,576]{3,2,1,0:T(4,128)(2,1)} %broadcast_in_dim.7), calls=%async_computation | async-start | bytes 983040 | tf_op jit(solution)/shard_map/all_to_all | solution.py:81
  15.5 0.7 copy-start.3
  30.9 0.8 copy-start.1

commit v2 on v1

v2 whole, which is shorter than its diff:
```python
import math

import jax
import jax.numpy as jnp
from jax import lax
from jax.experimental import pallas as pl
from jax.experimental.pallas import tpu as pltpu
from jax.sharding import PartitionSpec as P

LATENT = 512
ROPE = 64
BLOCK = 64
LANES = 128
CHUNKS = LATENT // LANES
GRANT = 12 * 1024 * 1024

score_scale = 1.0 / math.sqrt(192.0)
very_low = -1e30
f32 = jnp.float32
bf16 = jnp.bfloat16


def pieces(value):
    high = value.astype(bf16).astype(f32)
    rest = value - high
    middle = rest.astype(bf16).astype(f32)
    return high, middle, rest - middle


def spread_kernel(query_ref, out_ref):
    steps, heads_dev, _ = query_ref.shape
    packed = []
    for t in range(steps):
        for c in range(CHUNKS):
            packed.append(query_ref[t, :, c * LANES : (c + 1) * LANES])
    rotary = [query_ref[t, :, LATENT:] for t in range(steps)]
    rotary.append(jnp.zeros_like(rotary[0]))
    for t in range(0, len(rotary), 2):
        packed.append(jnp.concatenate([rotary[t], rotary[t + 1]], axis=1))
    for k, piece in enumerate(packed):
        out_ref[:, k * heads_dev : (k + 1) * heads_dev, :] = jnp.broadcast_to(
            piece[None], (out_ref.shape[0], heads_dev, LANES)
        )


def attend_kernel(usable_ref, query_ref, cache_ref, out_ref, rows_ref, rotary_ref, sums_ref):
    shards = query_ref.shape[0]
    steps, heads, _ = rows_ref.shape
    heads_dev = heads // shards
    for s in range(shards):
        span = slice(s * heads_dev, (s + 1) * heads_dev)
        for t in range(steps):
            for c in range(CHUNKS):
                k = (t * CHUNKS + c) * heads_dev
                rows_ref[t, span, c * LANES : (c + 1) * LANES] = query_ref[s, k : k + heads_dev, :]
        for pair in range(rotary_ref.shape[0]):
            k = (steps * CHUNKS + pair) * heads_dev
            rotary_ref[pair, span, :] = query_ref[s, k : k + heads_dev, :]
    latent = cache_ref[:LATENT, :]
    rotary_keys = cache_ref[LATENT:, :]
    lane = lax.broadcasted_iota(jnp.int32, (heads, LANES), 1)
    stats = jnp.zeros((heads, LANES), f32)
    for t in range(steps):
        usable = usable_ref[t : t + 1, :] > 0.0
        rotary = rotary_ref[t // 2, :, (t % 2) * ROPE : (t % 2 + 1) * ROPE]
        scores = jnp.dot(rows_ref[t], latent, preferred_element_type=f32)
        scores = scores + jnp.dot(rotary, rotary_keys, preferred_element_type=f32)
        scores = jnp.where(usable, scores * score_scale, very_low)
        peak = jnp.max(scores, axis=1, keepdims=True)
        raw = jnp.where(usable, jnp.exp(scores - peak), 0.0)
        total = jnp.sum(raw, axis=1, keepdims=True)
        weighted = lax.dot_general(
            raw.astype(bf16), latent, (((1,), (1,)), ((), ())), preferred_element_type=f32
        )
        sums_ref[:, t * LATENT : (t + 1) * LATENT] = weighted.astype(bf16)
        for k, piece in enumerate(pieces(peak) + pieces(total)):
            stats = jnp.where(lane == t * 6 + k, piece, stats)
    sums_ref[:, steps * LATENT :] = stats.astype(bf16)
    for s in range(shards):
        for k in range(out_ref.shape[1]):
            out_ref[s, k] = sums_ref[
                s * heads_dev : (s + 1) * heads_dev, k * LANES : (k + 1) * LANES
            ]


def merge_kernel(parts_ref, value_ref, out_ref):
    shards, _, heads_dev, _ = parts_ref.shape
    requests, steps, _, _ = out_ref.shape
    stats = parts_ref[:, steps * CHUNKS].astype(f32)
    row = lax.broadcasted_iota(jnp.int32, (heads_dev, LANES), 0)
    for t in range(steps):
        k = t * 6
        peak = stats[:, :, k : k + 1] + stats[:, :, k + 1 : k + 2] + stats[:, :, k + 2 : k + 3]
        total = stats[:, :, k + 3 : k + 4] + stats[:, :, k + 4 : k + 5] + stats[:, :, k + 5 : k + 6]
        factor = jnp.exp(peak - jnp.max(peak, axis=0, keepdims=True))
        whole = jnp.sum(total * factor, axis=0)
        wide = jnp.broadcast_to(factor, (shards, heads_dev, LANES))
        latent_out = []
        for c in range(CHUNKS):
            part = parts_ref[:, t * CHUNKS + c].astype(f32)
            latent_out.append((jnp.sum(part * wide, axis=0) / whole).astype(bf16))
        latent_out = jnp.concatenate(latent_out, axis=1)
        heads = jnp.zeros((heads_dev, LANES), f32)
        for h in range(heads_dev):
            product = jnp.dot(latent_out, value_ref[h], preferred_element_type=f32)
            heads = jnp.where(row == h, product, heads)
        out_ref[:, t] = jnp.broadcast_to(heads.astype(bf16)[None], (requests, heads_dev, LANES))


def project_kernel(heads_ref, weight_ref, out_ref, flat_ref, wide_ref):
    requests, steps, heads_dev, _ = heads_ref.shape
    queries = requests * steps
    shards, half, width = out_ref.shape
    for q in range(queries):
        flat_ref[q * heads_dev : (q + 1) * heads_dev, :] = heads_ref[q // steps, q % steps]
    every = flat_ref[...]
    out_row = lax.broadcasted_iota(jnp.int32, (width, queries * heads_dev), 0)
    in_row = lax.broadcasted_iota(jnp.int32, (width, queries * heads_dev), 1)
    source = jnp.where(out_row < queries, out_row, out_row - queries) * heads_dev
    mixed = jnp.zeros(wide_ref.shape, f32)
    for h in range(heads_dev):
        pick = jnp.where(in_row == source + h, 1.0, 0.0).astype(bf16)
        of_head = jnp.dot(pick, every, preferred_element_type=f32).astype(bf16)
        mixed = mixed + lax.dot_general(
            weight_ref[:, h * LANES : (h + 1) * LANES],
            of_head,
            (((1,), (1,)), ((), ())),
            preferred_element_type=f32,
        )
    wide_ref[...] = mixed
    lane = lax.broadcasted_iota(jnp.int32, (half, width), 1)
    for s in range(shards):
        first = wide_ref[2 * half * s : 2 * half * s + half, :]
        second = wide_ref[2 * half * s + half : 2 * half * (s + 1), :]
        out_ref[s] = jnp.where(lane < queries, first, second).astype(bf16)


def finish_kernel(parts_ref, out_ref):
    _, half, width = parts_ref.shape
    total = jnp.sum(parts_ref[...].astype(f32), axis=0)
    out_ref[:half, :] = total[:, : width // 2].astype(bf16)
    out_ref[half:, :] = total[:, width // 2 :].astype(bf16)


def exchanged(value, axis):
    return lax.all_to_all(value, axis, 0, 0, tiled=True)


def kernel(fn, shape, name, scratch=(), dtype=bf16):
    return pl.pallas_call(
        fn,
        out_shape=jax.ShapeDtypeStruct(shape, dtype),
        scratch_shapes=[pltpu.VMEM(*s) for s in scratch],
        compiler_params=pltpu.CompilerParams(vmem_limit_bytes=GRANT),
        name=name,
    )


def body(latent_cache, queries, chosen, position, w_value, w_out):
    cache_len, key_width = latent_cache.shape[1:]
    _, steps, heads_dev, _ = queries.shape
    shards = lax.axis_size("seq")
    requests = lax.axis_size("req")
    shard_index = lax.axis_index("seq")
    heads = shards * heads_dev

    packed_rows = (steps * CHUNKS + (steps + 1) // 2) * heads_dev
    query_all = kernel(spread_kernel, (shards, packed_rows, LANES), "spread")(queries[0])
    query_all = exchanged(query_all, "seq")

    rows = shard_index * cache_len + jnp.arange(cache_len, dtype=jnp.int32)
    usable = jnp.any(chosen[0][:, :, None] == rows // BLOCK, axis=1) & (rows < position[0])
    parts = kernel(
        attend_kernel,
        (shards, steps * CHUNKS + 1, heads_dev, LANES),
        "attend",
        (
            ((steps, heads, LATENT), bf16),
            (((steps + 1) // 2, heads, LANES), bf16),
            ((heads, steps * LATENT + LANES), bf16),
        ),
    )(usable.astype(f32), query_all, latent_cache[0].T)
    parts = exchanged(parts, "seq")
    head_out = kernel(merge_kernel, (requests, steps, heads_dev, w_value.shape[2]), "merge")(
        parts, w_value
    )
    head_out = exchanged(head_out, "req")
    features = w_out.shape[1]
    count = requests * steps
    mixed = kernel(
        project_kernel,
        (shards, features // shards // 2, 2 * count),
        "project",
        (((count * heads_dev, LANES), bf16), ((features, 2 * count), f32)),
    )(head_out, w_out.T)
    mixed = exchanged(mixed, "seq")
    return kernel(finish_kernel, (features // shards, count), "finish")(mixed)


def solution(mesh):
    return jax.shard_map(
        body,
        mesh=mesh,
        in_specs=(
            P("req", "seq", None),
            P("req", None, "seq", None),
            P("req", None, None),
            P("req"),
            P("seq", None, None),
            P("seq", "req"),
        ),
        out_specs=P(("req", "seq"), None),
        check_vma=False,
    )
```

time: 93.6 us -> 83.6 us (0.89)
  local copies, waits for them, and re-layouts: 6.75 us -> 0.75 us
  Pallas kernels: 6.21 us -> 4.45 us
  other arithmetic: 1.75 us -> 0.14 us
  blocking collectives: 51.2 us -> 49.6 us
  waiting for transfers between devices: 12.2 us -> 13.6 us
    broadcast_in_dim x2 -> x0, local copies, waits for them, and re-layouts: 2.39 us -> none  [the longest x1 1.68 us: body(): jnp.broadcast_to(queries, (shards, steps, heads_dev, key_width))]
    unnamed x12 -> x11, local copies, waits for them, and re-layouts: 2.8 us -> 0.75 us
    pallas_call x2 -> x5, Pallas kernels: 6.21 us -> 4.45 us  [the longest x1 1.48 us: body(): kernel(attend_kernel, (shards, steps * CHUNKS + 1, heads_dev, LANES), 'at...]
    all_to_all x3, blocking collectives: 51.2 us -> 49.6 us  [exchanged(): return lax.all_to_all(value, axis, 0, 0, tiled=True)]
    reshape x4 -> x0, local copies, waits for them, and re-layouts: 1.42 us -> none  [the longest x2 0.69 us: body(): mixed = exchanged(partial.reshape(shards, 1, -1), 'seq')]
    all_to_all x1, waiting for transfers between devices: 12.2 us -> 13.6 us  [exchanged(): return lax.all_to_all(value, axis, 0, 0, tiled=True)]
  transfers between devices with their start and end apart: 1 -> 1, of which waited for: 1 -> 1; matrix products, arithmetic and copies ran while one was open for 2% -> 0% of each run, Pallas kernels for 0% -> 0%
where the time goes in v2:
time: 83.6 us; the launch traced here: 83.2 us
  blocking collectives  49.6 us (59%)
  starting transfers between devices  13.8 us (17%)
  waiting for transfers between devices  13.6 us (16%)
  Pallas kernels  4.45 us (5%)
    all_to_all x3, blocking collectives, exchanged(): return lax.all_to_all(value, axis, 0, 0, tiled=True)  49.6 us
    all_to_all x1, starting transfers between devices, exchanged(): return lax.all_to_all(value, axis, 0, 0, tiled=True)  13.8 us
    all_to_all x1, waiting for transfers between devices, exchanged(): return lax.all_to_all(value, axis, 0, 0, tiled=True)  13.6 us
  transfers between devices with their start and end apart: 1, of which 1 were waited for; matrix products, arithmetic and copies ran while one was open for 0% of the time, Pallas kernels for 0%

profile of v2, /device:TPU:1, one launch (start us, length us, event | category | flops | bytes accessed | tf_op | source)
XLA Modules:
  0.0 83.2 jit_solution(3237219703315637669)
XLA Ops:
  0.0 0.0 copy-start.3
  0.0 0.7 copy-done.3
  0.7 0.9 %spread.1 = bf16[32,56,128]{2,1,0:T(8,128)(2,1)} custom-call(bf16[3,4,576]{2,1,0:T(4,128)(2,1)S(1)} %bitcast.12), custom_call_target="tpu_custom_call" | custom-call | tf_op jit(solution)/shard_map/spread/pallas_call | solution.py:168
  1.6 0.0 copy-start
  1.6 13.8 %all-to-all-start = ((bf16[32,56,128]{2,1,0:T(8,128)(2,1)}), bf16[32,56,128]{2,1,0:T(8,128)(2,1)S(1)}, u32[]{:S(2)}, u32[]{:S(2)}) async-start(bf16[32,56,128]{2,1,0:T(8,128)(2,1)} %spread.1), calls=%async_computation | async-start | bytes 917504 | tf_op jit(solution)/shard_map/all_to_all | solution.py:146
  15.5 0.0 copy-start.4
  16.2 0.0 copy-done.4
  16.2 0.1 compare_reduce_fusion
  16.3 13.6 %all-to-all-done.query_ref = bf16[32,56,128]{2,1,0:T(8,128)(2,1)S(1)} async-done(((bf16[32,56,128]{2,1,0:T(8,128)(2,1)}), bf16[32,56,128]{2,1,0:T(8,128)(2,1)S(1)}, u32[]{:S(2)}, u32[]{:S(2)}) %all-to-all-start) | async-done | bytes 458784 | tf_op jit(solution)/shard_map/all_to_all | solution.py:146
  29.9 0.0 copy-done
  29.9 1.5 %attend.1 = bf16[32,13,4,128]{3,2,1,0:T(4,128)(2,1)S(1)} custom-call(f32[3,512]{1,0:T(4,128)S(1)} %and_convert_fusion.usable_ref, bf16[32,56,128]{2,1,0:T(8,128)(2,1)S(1)} %all-to-all-done.query_ref, bf16[576,512]{1,0:T(8,128)(2,1)S(1)} %bitcast.10), custom_call_target="tpu_custom_call" | custom-call | tf_op jit(solution)/shard_map/attend/pallas_call | solution.py:173
  31.4 0.0 copy-start.1
  31.4 19.1 %all_to_all.20.parts_ref = bf16[32,13,4,128]{3,2,1,0:T(4,128)(2,1)S(1)} all-to-all(bf16[32,13,4,128]{3,2,1,0:T(4,128)(2,1)S(1)} %attend.1), channel_id=1, replica_groups=mesh['req'=16,'seq'=32] {'seq'}, dimensions={0} | all-to-all | bytes 851968 | tf_op jit(solution)/shard_map/all_to_all | solution.py:146
  50.6 0.0 copy-done.1
  50.6 0.0 copy-start.2
  50.6 0.7 merge.1
  51.3 17.9 %all_to_all.21.heads_ref = bf16[16,3,4,128]{3,2,1,0:T(4,128)(2,1)S(1)} all-to-all(bf16[16,3,4,128]{3,2,1,0:T(4,128)(2,1)S(1)} %merge.1), channel_id=1, replica_groups=mesh['req'=16,'seq'=32] {'req'}, dimensions={0} | all-to-all | bytes 98304 | tf_op jit(solution)/shard_map/all_to_all | solution.py:146
  69.1 0.0 copy-done.2
  69.1 0.7 project.1
  69.8 12.6 %all_to_all.22.parts_ref = bf16[32,7,96]{2,1,0:T(8,128)(2,1)S(1)} all-to-all(bf16[32,7,96]{2,1,0:T(8,128)(2,1)S(1)} %project.1), channel_id=1, replica_groups=mesh['req'=16,'seq'=32] {'seq'}, dimensions={0} | all-to-all | bytes 86016 | tf_op jit(solution)/shard_map/all_to_all | solution.py:146
  82.5 0.7 finish.1
  (4 shorter events, 0.0 us)
Async XLA Ops:
  0.0 0.7 copy-start.3
  1.6 28.3 %copy-start = (bf16[1,512,576]{1,2,0:T(8,128)(2,1)S(1)}, bf16[1,512,576]{1,2,0:T(8,128)(2,1)}, u32[]{:S(2)}) copy-start(bf16[1,512,576]{1,2,0:T(8,128)(2,1)} %param.6) | copy-start | bytes 1769476
  1.6 28.3 %all-to-all-start = ((bf16[32,56,128]{2,1,0:T(8,128)(2,1)}), bf16[32,56,128]{2,1,0:T(8,128)(2,1)S(1)}, u32[]{:S(2)}, u32[]{:S(2)}) async-start(bf16[32,56,128]{2,1,0:T(8,128)(2,1)} %spread.1), calls=%async_computation | async-start | bytes 917504 | tf_op jit(solution)/shard_map/all_to_all | solution.py:146
  15.5 0.7 copy-start.4
  31.4 19.2 %copy-start.1 = (bf16[4,512,128]{2,1,0:T(8,128)(2,1)S(1)}, bf16[4,512,128]{2,1,0:T(8,128)(2,1)}, u32[]{:S(2)}) copy-start(bf16[4,512,128]{2,1,0:T(8,128)(2,1)} %value_ref.1) | copy-start | bytes 1572868
  50.6 18.6 %copy-start.2 = (bf16[512,448]{0,1:T(8,128)(2,1)S(1)}, bf16[512,448]{0,1:T(8,128)(2,1)}, u32[]{:S(2)}) copy-start(bf16[512,448]{0,1:T(8,128)(2,1)} %param.11) | copy-start | bytes 1376260

commit v3 on v2

--- a/solution.py
+++ b/solution.py
@@ -27,7 +27,17 @@
     return high, middle, rest - middle
 
 
-def spread_kernel(query_ref, out_ref):
+def spread_kernel(query_hbm, chosen_hbm, position_ref, out_ref, usable_ref, query_ref, chosen_ref, sems):
+    copies = [
+        pltpu.make_async_copy(source, target, sems.at[k])
+        for k, (source, target) in enumerate(
+            ((query_hbm, query_ref), (chosen_hbm, chosen_ref))
+        )
+    ]
+    for copy in copies:
+        copy.start()
+    for copy in copies:
+        copy.wait()
     steps, heads_dev, _ = query_ref.shape
     packed = []
     for t in range(steps):
@@ -41,6 +51,15 @@
         out_ref[:, k * heads_dev : (k + 1) * heads_dev, :] = jnp.broadcast_to(
             piece[None], (out_ref.shape[0], heads_dev, LANES)
         )
+    cache_len = usable_ref.shape[1]
+    row = lax.axis_index("seq") * cache_len + lax.broadcasted_iota(jnp.int32, (1, cache_len), 1)
+    block = row // BLOCK
+    inside = row < position_ref[0]
+    for t in range(steps):
+        named = jnp.zeros((1, cache_len), jnp.bool_)
+        for k in range(chosen_ref.shape[2]):
+            named = named | (block == chosen_ref[t, :, k : k + 1])
+        usable_ref[t : t + 1, :] = jnp.where(named & inside, 1.0, 0.0)
 
 
 def attend_kernel(usable_ref, query_ref, cache_ref, out_ref, rows_ref, rotary_ref, sums_ref):
@@ -161,15 +180,30 @@
     _, steps, heads_dev, _ = queries.shape
     shards = lax.axis_size("seq")
     requests = lax.axis_size("req")
-    shard_index = lax.axis_index("seq")
     heads = shards * heads_dev
 
     packed_rows = (steps * CHUNKS + (steps + 1) // 2) * heads_dev
-    query_all = kernel(spread_kernel, (shards, packed_rows, LANES), "spread")(queries[0])
+    query_all, usable = pl.pallas_call(
+        spread_kernel,
+        out_shape=(
+            jax.ShapeDtypeStruct((shards, packed_rows, LANES), bf16),
+            jax.ShapeDtypeStruct((steps, cache_len), f32),
+        ),
+        in_specs=[pl.BlockSpec(memory_space=pltpu.HBM)] * 2
+        + [pl.BlockSpec(memory_space=pltpu.SMEM)],
+        scratch_shapes=[
+            pltpu.VMEM((steps, heads_dev, key_width), bf16),
+            pltpu.VMEM((steps, 1, chosen.shape[2]), jnp.int32),
+            pltpu.SemaphoreType.DMA((2,)),
+        ],
+        compiler_params=pltpu.CompilerParams(vmem_limit_bytes=GRANT),
+        name="spread",
+    )(
+        pltpu.with_memory_space_constraint(queries[0], pltpu.HBM),
+        pltpu.with_memory_space_constraint(jnp.swapaxes(chosen, 0, 1), pltpu.HBM),
+        position,
+    )
     query_all = exchanged(query_all, "seq")
-
-    rows = shard_index * cache_len + jnp.arange(cache_len, dtype=jnp.int32)
-    usable = jnp.any(chosen[0][:, :, None] == rows // BLOCK, axis=1) & (rows < position[0])
     parts = kernel(
         attend_kernel,
         (shards, steps * CHUNKS + 1, heads_dev, LANES),
@@ -179,7 +213,7 @@
             (((steps + 1) // 2, heads, LANES), bf16),
             ((heads, steps * LATENT + LANES), bf16),
         ),
-    )(usable.astype(f32), query_all, latent_cache[0].T)
+    )(usable, query_all, latent_cache[0].T)
     parts = exchanged(parts, "seq")
     head_out = kernel(merge_kernel, (requests, steps, heads_dev, w_value.shape[2]), "merge")(
         parts, w_value

time: 83.6 us -> 83.4 us (level)
  blocking collectives: 49.6 us -> 77.6 us
  starting transfers between devices: 13.8 us -> 0 us
  waiting for transfers between devices: 13.6 us -> 0 us
    all_to_all x3 -> x4, blocking collectives: 49.6 us -> 77.6 us  [exchanged(): return lax.all_to_all(value, axis, 0, 0, tiled=True)]
    all_to_all x1 -> x0, starting transfers between devices: 13.8 us -> none  [exchanged(): return lax.all_to_all(value, axis, 0, 0, tiled=True)]
    all_to_all x1 -> x0, waiting for transfers between devices: 13.6 us -> none  [exchanged(): return lax.all_to_all(value, axis, 0, 0, tiled=True)]
  transfers between devices with their start and end apart: 1 -> 0, of which waited for: 1 -> 0; matrix products, arithmetic and copies ran while one was open for 0% -> 0% of each run, Pallas kernels for 0% -> 0%
where the time goes in v3:
time: 83.4 us; the launch traced here: 83.1 us
  blocking collectives  77.6 us (93%)
  Pallas kernels  4.72 us (6%)
    all_to_all x4, blocking collectives, exchanged(): return lax.all_to_all(value, axis, 0, 0, tiled=True)  77.6 us

profile of v3, /device:TPU:1, one launch (start us, length us, event | category | flops | bytes accessed | tf_op | source)
XLA Modules:
  0.0 83.1 jit_solution(2119738511976037897)
XLA Ops:
  0.0 0.0 copy-start
  0.7 1.2 %spread.1 = (bf16[32,56,128]{2,1,0:T(8,128)(2,1)S(1)}, f32[3,512]{1,0:T(4,128)S(1)}) custom-call(bf16[3,4,576]{2,1,0:T(4,128)(2,1)} %bitcast.8, s32[3,1,32]{2,1,0:T(1,128)} %bitcast.9, s32[1]{0:T(128)S(6)} %copy.7.position_ref), custom_call_target="tpu_custom_call" | custom-call | tf_op jit(solution)/shard_map/spread/pallas_call | solution.py:186
  1.9 28.0 %all_to_all.20.query_ref = bf16[32,56,128]{2,1,0:T(8,128)(2,1)S(1)} all-to-all(bf16[32,56,128]{2,1,0:T(8,128)(2,1)S(1)} %get-tuple-element.8), channel_id=1, replica_groups=mesh['req'=16,'seq'=32] {'seq'}, dimensions={0} | all-to-all | bytes 917504 | tf_op jit(solution)/shard_map/all_to_all | solution.py:165
  29.9 0.0 copy-done
  29.9 1.5 %attend.1 = bf16[32,13,4,128]{3,2,1,0:T(4,128)(2,1)S(1)} custom-call(f32[3,512]{1,0:T(4,128)S(1)} %get-tuple-element.7.usable_ref, bf16[32,56,128]{2,1,0:T(8,128)(2,1)S(1)} %all_to_all.20.query_ref, bf16[576,512]{1,0:T(8,128)(2,1)S(1)} %bitcast.6), custom_call_target="tpu_custom_call" | custom-call | tf_op jit(solution)/shard_map/attend/pallas_call | solution.py:207
  31.4 0.0 copy-start.1
  31.4 19.1 %all_to_all.21.parts_ref = bf16[32,13,4,128]{3,2,1,0:T(4,128)(2,1)S(1)} all-to-all(bf16[32,13,4,128]{3,2,1,0:T(4,128)(2,1)S(1)} %attend.1), channel_id=1, replica_groups=mesh['req'=16,'seq'=32] {'seq'}, dimensions={0} | all-to-all | bytes 851968 | tf_op jit(solution)/shard_map/all_to_all | solution.py:165
  50.5 0.0 copy-done.1
  50.5 0.0 copy-start.2
  50.5 0.7 merge.1
  51.2 17.9 %all_to_all.22.heads_ref = bf16[16,3,4,128]{3,2,1,0:T(4,128)(2,1)S(1)} all-to-all(bf16[16,3,4,128]{3,2,1,0:T(4,128)(2,1)S(1)} %merge.1), channel_id=1, replica_groups=mesh['req'=16,'seq'=32] {'req'}, dimensions={0} | all-to-all | bytes 98304 | tf_op jit(solution)/shard_map/all_to_all | solution.py:165
  69.1 0.0 copy-done.2
  69.1 0.7 project.1
  69.8 12.6 %all_to_all.23.parts_ref = bf16[32,7,96]{2,1,0:T(8,128)(2,1)S(1)} all-to-all(bf16[32,7,96]{2,1,0:T(8,128)(2,1)S(1)} %project.1), channel_id=1, replica_groups=mesh['req'=16,'seq'=32] {'seq'}, dimensions={0} | all-to-all | bytes 86016 | tf_op jit(solution)/shard_map/all_to_all | solution.py:165
  82.4 0.7 finish.1
Async XLA Ops:
  0.0 29.9 %copy-start = (bf16[1,512,576]{1,2,0:T(8,128)(2,1)S(1)}, bf16[1,512,576]{1,2,0:T(8,128)(2,1)}, u32[]{:S(2)}) copy-start(bf16[1,512,576]{1,2,0:T(8,128)(2,1)} %param.6) | copy-start | bytes 1769476
  31.4 19.2 %copy-start.1 = (bf16[4,512,128]{2,1,0:T(8,128)(2,1)S(1)}, bf16[4,512,128]{2,1,0:T(8,128)(2,1)}, u32[]{:S(2)}) copy-start(bf16[4,512,128]{2,1,0:T(8,128)(2,1)} %value_ref.1) | copy-start | bytes 1572868
  50.5 18.6 %copy-start.2 = (bf16[512,448]{0,1:T(8,128)(2,1)S(1)}, bf16[512,448]{0,1:T(8,128)(2,1)}, u32[]{:S(2)}) copy-start(bf16[512,448]{0,1:T(8,128)(2,1)} %param.11) | copy-start | bytes 1376260

commit v4 on v3

--- a/solution.py
+++ b/solution.py
@@ -52,78 +52,91 @@
             piece[None], (out_ref.shape[0], heads_dev, LANES)
         )
     cache_len = usable_ref.shape[1]
-    row = lax.axis_index("seq") * cache_len + lax.broadcasted_iota(jnp.int32, (1, cache_len), 1)
-    block = row // BLOCK
-    inside = row < position_ref[0]
-    for t in range(steps):
-        named = jnp.zeros((1, cache_len), jnp.bool_)
-        for k in range(chosen_ref.shape[2]):
-            named = named | (block == chosen_ref[t, :, k : k + 1])
-        usable_ref[t : t + 1, :] = jnp.where(named & inside, 1.0, 0.0)
-
-
-def attend_kernel(usable_ref, query_ref, cache_ref, out_ref, rows_ref, rotary_ref, sums_ref):
+    blocks = cache_len // BLOCK
+    first = lax.axis_index("seq") * cache_len
+    column = lax.broadcasted_iota(jnp.int32, (blocks, cache_len), 1)
+    mine = column // BLOCK == lax.broadcasted_iota(jnp.int32, (blocks, cache_len), 0)
+    mine = mine & (first + column < position_ref[0])
+    wanted = chosen_ref.shape[2]
+    block = first // BLOCK + lax.broadcasted_iota(jnp.int32, (blocks, wanted), 0)
+    for t in range(steps):
+        named = jnp.where(chosen_ref[t] == block, 1.0, 0.0)
+        named = jnp.max(named, axis=1, keepdims=True)
+        usable_ref[t : t + 1, :] = jnp.max(jnp.where(mine, named, 0.0), axis=0, keepdims=True)
+
+
+def attend_kernel(usable_ref, query_ref, cache_ref, out_ref, rotary_ref, stats_ref, *work):
     shards = query_ref.shape[0]
-    steps, heads, _ = rows_ref.shape
+    steps = usable_ref.shape[0]
+    heads = rotary_ref.shape[1]
     heads_dev = heads // shards
-    for s in range(shards):
-        span = slice(s * heads_dev, (s + 1) * heads_dev)
-        for t in range(steps):
-            for c in range(CHUNKS):
-                k = (t * CHUNKS + c) * heads_dev
-                rows_ref[t, span, c * LANES : (c + 1) * LANES] = query_ref[s, k : k + heads_dev, :]
-        for pair in range(rotary_ref.shape[0]):
-            k = (steps * CHUNKS + pair) * heads_dev
-            rotary_ref[pair, span, :] = query_ref[s, k : k + heads_dev, :]
+    spans = [slice(s * heads_dev, (s + 1) * heads_dev) for s in range(shards)]
+    for pair in range(rotary_ref.shape[0]):
+        k = (steps * CHUNKS + pair) * heads_dev
+        for s in range(shards):
+            rotary_ref[pair, spans[s], :] = query_ref[s, k : k + heads_dev, :]
     latent = cache_ref[:LATENT, :]
     rotary_keys = cache_ref[LATENT:, :]
     lane = lax.broadcasted_iota(jnp.int32, (heads, LANES), 1)
+    slot = lane % (2 * steps)
     stats = jnp.zeros((heads, LANES), f32)
     for t in range(steps):
-        usable = usable_ref[t : t + 1, :] > 0.0
+        rows_ref, sums_ref = work[2 * t], work[2 * t + 1]
+        for c in range(CHUNKS):
+            k = (t * CHUNKS + c) * heads_dev
+            for s in range(shards):
+                rows_ref[spans[s], c * LANES : (c + 1) * LANES] = query_ref[s, k : k + heads_dev, :]
         rotary = rotary_ref[t // 2, :, (t % 2) * ROPE : (t % 2 + 1) * ROPE]
-        scores = jnp.dot(rows_ref[t], latent, preferred_element_type=f32)
+        scores = jnp.dot(rows_ref[...], latent, preferred_element_type=f32)
         scores = scores + jnp.dot(rotary, rotary_keys, preferred_element_type=f32)
-        scores = jnp.where(usable, scores * score_scale, very_low)
+        scores = jnp.where(usable_ref[t : t + 1, :] > 0.0, scores, very_low)
         peak = jnp.max(scores, axis=1, keepdims=True)
-        raw = jnp.where(usable, jnp.exp(scores - peak), 0.0)
+        raw = jnp.exp2((scores - peak) * (score_scale * math.log2(math.e)))
         total = jnp.sum(raw, axis=1, keepdims=True)
-        weighted = lax.dot_general(
+        sums_ref[...] = lax.dot_general(
             raw.astype(bf16), latent, (((1,), (1,)), ((), ())), preferred_element_type=f32
-        )
-        sums_ref[:, t * LATENT : (t + 1) * LATENT] = weighted.astype(bf16)
-        for k, piece in enumerate(pieces(peak) + pieces(total)):
-            stats = jnp.where(lane == t * 6 + k, piece, stats)
-    sums_ref[:, steps * LATENT :] = stats.astype(bf16)
+        ).astype(bf16)
+        stats = jnp.where(slot == 2 * t, peak * score_scale, stats)
+        stats = jnp.where(slot == 2 * t + 1, total, stats)
+        for c in range(CHUNKS):
+            for s in range(shards):
+                out_ref[s, t * CHUNKS + c] = sums_ref[spans[s], c * LANES : (c + 1) * LANES]
+    high, middle, low = pieces(stats)
+    stats = jnp.where(lane < 2 * steps, high, jnp.where(lane < 4 * steps, middle, low))
+    stats_ref[...] = stats.astype(bf16)
     for s in range(shards):
-        for k in range(out_ref.shape[1]):
-            out_ref[s, k] = sums_ref[
-                s * heads_dev : (s + 1) * heads_dev, k * LANES : (k + 1) * LANES
-            ]
+        out_ref[s, steps * CHUNKS] = stats_ref[spans[s], :]
 
 
 def merge_kernel(parts_ref, value_ref, out_ref):
     shards, _, heads_dev, _ = parts_ref.shape
     requests, steps, _, _ = out_ref.shape
     stats = parts_ref[:, steps * CHUNKS].astype(f32)
-    row = lax.broadcasted_iota(jnp.int32, (heads_dev, LANES), 0)
-    for t in range(steps):
-        k = t * 6
-        peak = stats[:, :, k : k + 1] + stats[:, :, k + 1 : k + 2] + stats[:, :, k + 2 : k + 3]
-        total = stats[:, :, k + 3 : k + 4] + stats[:, :, k + 4 : k + 5] + stats[:, :, k + 5 : k + 6]
+    latent_out = []
+    for t in range(steps):
+        peak, total = (
+            stats[:, :, k : k + 1]
+            + stats[:, :, k + 2 * steps : k + 2 * steps + 1]
+            + stats[:, :, k + 4 * steps : k + 4 * steps + 1]
+            for k in (2 * t, 2 * t + 1)
+        )
         factor = jnp.exp(peak - jnp.max(peak, axis=0, keepdims=True))
         whole = jnp.sum(total * factor, axis=0)
         wide = jnp.broadcast_to(factor, (shards, heads_dev, LANES))
-        latent_out = []
+        chunks = []
         for c in range(CHUNKS):
             part = parts_ref[:, t * CHUNKS + c].astype(f32)
-            latent_out.append((jnp.sum(part * wide, axis=0) / whole).astype(bf16))
-        latent_out = jnp.concatenate(latent_out, axis=1)
-        heads = jnp.zeros((heads_dev, LANES), f32)
-        for h in range(heads_dev):
-            product = jnp.dot(latent_out, value_ref[h], preferred_element_type=f32)
-            heads = jnp.where(row == h, product, heads)
-        out_ref[:, t] = jnp.broadcast_to(heads.astype(bf16)[None], (requests, heads_dev, LANES))
+            chunks.append(jnp.sum(part * wide, axis=0) / whole)
+        latent_out.append(jnp.concatenate(chunks, axis=1))
+    latent_out = jnp.concatenate(latent_out, axis=0).astype(bf16)
+    row = lax.broadcasted_iota(jnp.int32, (steps * heads_dev, LANES), 0) % heads_dev
+    heads = jnp.zeros((steps * heads_dev, LANES), f32)
+    for h in range(heads_dev):
+        product = jnp.dot(latent_out, value_ref[h], preferred_element_type=f32)
+        heads = jnp.where(row == h, product, heads)
+    for t in range(steps):
+        mine = heads[t * heads_dev : (t + 1) * heads_dev, :].astype(bf16)
+        out_ref[:, t] = jnp.broadcast_to(mine[None], (requests, heads_dev, LANES))
 
 
 def project_kernel(heads_ref, weight_ref, out_ref, flat_ref, wide_ref):
@@ -209,9 +222,9 @@
         (shards, steps * CHUNKS + 1, heads_dev, LANES),
         "attend",
         (
-            ((steps, heads, LATENT), bf16),
             (((steps + 1) // 2, heads, LANES), bf16),
-            ((heads, steps * LATENT + LANES), bf16),
+            ((heads, LANES), bf16),
+            *(((heads, LATENT), bf16),) * (2 * steps),
         ),
     )(usable, query_all, latent_cache[0].T)
     parts = exchanged(parts, "seq")

time: 83.4 us -> 83.1 us (level)
  no operation moved by 1% of the time
where the time goes in v4:
time: 83.1 us; the launch traced here: 82.8 us
  blocking collectives  77.6 us (93%)
  Pallas kernels  4.42 us (5%)
    all_to_all x4, blocking collectives, exchanged(): return lax.all_to_all(value, axis, 0, 0, tiled=True)  77.6 us

profile of v4, /device:TPU:1, one launch (start us, length us, event | category | flops | bytes accessed | tf_op | source)
XLA Modules:
  0.0 82.8 jit_solution(18154770038023031354)
XLA Ops:
  0.0 0.0 copy-start
  0.7 0.9 %spread.1 = (bf16[32,56,128]{2,1,0:T(8,128)(2,1)S(1)}, f32[3,512]{1,0:T(4,128)S(1)}) custom-call(bf16[3,4,576]{2,1,0:T(4,128)(2,1)} %bitcast.8, s32[3,1,32]{2,1,0:T(1,128)} %bitcast.9, s32[1]{0:T(128)S(6)} %copy.7.position_ref), custom_call_target="tpu_custom_call" | custom-call | tf_op jit(solution)/shard_map/spread/pallas_call | solution.py:199
  1.6 28.0 %all_to_all.20.query_ref = bf16[32,56,128]{2,1,0:T(8,128)(2,1)S(1)} all-to-all(bf16[32,56,128]{2,1,0:T(8,128)(2,1)S(1)} %get-tuple-element.8), channel_id=1, replica_groups=mesh['req'=16,'seq'=32] {'seq'}, dimensions={0} | all-to-all | bytes 917504 | tf_op jit(solution)/shard_map/all_to_all | solution.py:178
  29.6 0.0 copy-done
  29.6 1.5 %attend.1 = bf16[32,13,4,128]{3,2,1,0:T(4,128)(2,1)S(1)} custom-call(f32[3,512]{1,0:T(4,128)S(1)} %get-tuple-element.7.usable_ref, bf16[32,56,128]{2,1,0:T(8,128)(2,1)S(1)} %all_to_all.20.query_ref, bf16[576,512]{1,0:T(8,128)(2,1)S(1)} %bitcast.6), custom_call_target="tpu_custom_call" | custom-call | tf_op jit(solution)/shard_map/attend/pallas_call | solution.py:220
  31.0 0.0 copy-start.1
  31.1 19.2 %all_to_all.21.parts_ref = bf16[32,13,4,128]{3,2,1,0:T(4,128)(2,1)S(1)} all-to-all(bf16[32,13,4,128]{3,2,1,0:T(4,128)(2,1)S(1)} %attend.1), channel_id=1, replica_groups=mesh['req'=16,'seq'=32] {'seq'}, dimensions={0} | all-to-all | bytes 851968 | tf_op jit(solution)/shard_map/all_to_all | solution.py:178
  50.2 0.0 copy-done.1
  50.2 0.0 copy-start.2
  50.2 0.7 merge.1
  50.9 17.9 %all_to_all.22.heads_ref = bf16[16,3,4,128]{3,2,1,0:T(4,128)(2,1)S(1)} all-to-all(bf16[16,3,4,128]{3,2,1,0:T(4,128)(2,1)S(1)} %merge.1), channel_id=1, replica_groups=mesh['req'=16,'seq'=32] {'req'}, dimensions={0} | all-to-all | bytes 98304 | tf_op jit(solution)/shard_map/all_to_all | solution.py:178
  68.8 0.0 copy-done.2
  68.8 0.7 project.1
  69.5 12.6 %all_to_all.23.parts_ref = bf16[32,7,96]{2,1,0:T(8,128)(2,1)S(1)} all-to-all(bf16[32,7,96]{2,1,0:T(8,128)(2,1)S(1)} %project.1), channel_id=1, replica_groups=mesh['req'=16,'seq'=32] {'seq'}, dimensions={0} | all-to-all | bytes 86016 | tf_op jit(solution)/shard_map/all_to_all | solution.py:178
  82.1 0.7 finish.1
Async XLA Ops:
  0.0 29.6 %copy-start = (bf16[1,512,576]{1,2,0:T(8,128)(2,1)S(1)}, bf16[1,512,576]{1,2,0:T(8,128)(2,1)}, u32[]{:S(2)}) copy-start(bf16[1,512,576]{1,2,0:T(8,128)(2,1)} %param.6) | copy-start | bytes 1769476
  31.0 19.2 %copy-start.1 = (bf16[4,512,128]{2,1,0:T(8,128)(2,1)S(1)}, bf16[4,512,128]{2,1,0:T(8,128)(2,1)}, u32[]{:S(2)}) copy-start(bf16[4,512,128]{2,1,0:T(8,128)(2,1)} %value_ref.1) | copy-start | bytes 1572868
  50.2 18.6 %copy-start.2 = (bf16[512,448]{0,1:T(8,128)(2,1)S(1)}, bf16[512,448]{0,1:T(8,128)(2,1)}, u32[]{:S(2)}) copy-start(bf16[512,448]{0,1:T(8,128)(2,1)} %param.11) | copy-start | bytes 1376260

commit v5 on v4

v5 whole, which is shorter than its diff:
```python
import functools
import math

import jax
import jax.numpy as jnp
from jax import lax
from jax.experimental import pallas as pl
from jax.experimental.pallas import tpu as pltpu
from jax.sharding import PartitionSpec as P


LATENT = 512
ROPE = 64
BLOCK = 64
LANES = 128
CHUNKS = LATENT // LANES
STREAMS = ((0, 3),)
GRANT = 12 * 1024 * 1024

score_scale = 1.0 / math.sqrt(192.0)
very_low = -1e30
f32 = jnp.float32
bf16 = jnp.bfloat16


def pieces(value):
    high = value.astype(bf16).astype(f32)
    rest = value - high
    middle = rest.astype(bf16).astype(f32)
    return high, middle, rest - middle


def spread_kernel(query_hbm, *refs):
    *out_refs, query_ref, sem = refs
    copy = pltpu.make_async_copy(query_hbm, query_ref, sem)
    copy.start()
    copy.wait()
    for (begin, end), out_ref in zip(STREAMS, out_refs):
        packed = []
        for t in range(begin, end):
            for c in range(CHUNKS):
                packed.append(query_ref[t, :, c * LANES : (c + 1) * LANES])
        rotary = [query_ref[t, :, LATENT:] for t in range(begin, end)]
        if len(rotary) % 2:
            rotary.append(jnp.zeros_like(rotary[0]))
        for t in range(0, len(rotary), 2):
            packed.append(jnp.concatenate([rotary[t], rotary[t + 1]], axis=1))
        for k, piece in enumerate(packed):
            out_ref[:, k] = jnp.broadcast_to(piece[None], (out_ref.shape[0], *piece.shape))


def mark_kernel(chosen_ref, position_ref, usable_ref):
    steps, cache_len = usable_ref.shape
    blocks = cache_len // BLOCK
    first = lax.axis_index("seq") * cache_len
    column = lax.broadcasted_iota(jnp.int32, (blocks, cache_len), 1)
    mine = column // BLOCK == lax.broadcasted_iota(jnp.int32, (blocks, cache_len), 0)
    mine = mine & (first + column < position_ref[0])
    wanted = chosen_ref.shape[2]
    block = first // BLOCK + lax.broadcasted_iota(jnp.int32, (blocks, wanted), 0)
    for t in range(steps):
        named = jnp.where(chosen_ref[t] == block, 1.0, 0.0)
        named = jnp.max(named, axis=1, keepdims=True)
        usable_ref[t : t + 1, :] = jnp.max(jnp.where(mine, named, 0.0), axis=0, keepdims=True)


def attend_kernel(begin, usable_ref, query_ref, cache_ref, out_ref, rotary_ref, stats_ref, *work):
    shards = query_ref.shape[0]
    steps = len(work) // 2
    heads = rotary_ref.shape[1]
    heads_dev = heads // shards
    spans = [slice(s * heads_dev, (s + 1) * heads_dev) for s in range(shards)]
    for pair in range(rotary_ref.shape[0]):
        for s in range(shards):
            rotary_ref[pair, spans[s], :] = query_ref[s, steps * CHUNKS + pair]
    latent = cache_ref[:LATENT, :]
    rotary_keys = cache_ref[LATENT:, :]
    lane = lax.broadcasted_iota(jnp.int32, (heads, LANES), 1)
    slot = lane % (2 * steps)
    stats = jnp.zeros((heads, LANES), f32)
    for t in range(steps):
        rows_ref, sums_ref = work[2 * t], work[2 * t + 1]
        for c in range(CHUNKS):
            for s in range(shards):
                rows_ref[spans[s], c * LANES : (c + 1) * LANES] = query_ref[s, t * CHUNKS + c]
        rotary = rotary_ref[t // 2, :, (t % 2) * ROPE : (t % 2 + 1) * ROPE]
        scores = jnp.dot(rows_ref[...], latent, preferred_element_type=f32)
        scores = scores + jnp.dot(rotary, rotary_keys, preferred_element_type=f32)
        scores = jnp.where(usable_ref[begin + t : begin + t + 1, :] > 0.0, scores, very_low)
        peak = jnp.max(scores, axis=1, keepdims=True)
        raw = jnp.exp2((scores - peak) * (score_scale * math.log2(math.e)))
        total = jnp.sum(raw, axis=1, keepdims=True)
        sums_ref[...] = lax.dot_general(
            raw.astype(bf16), latent, (((1,), (1,)), ((), ())), preferred_element_type=f32
        ).astype(bf16)
        stats = jnp.where(slot == 2 * t, peak * score_scale, stats)
        stats = jnp.where(slot == 2 * t + 1, total, stats)
        for c in range(CHUNKS):
            for s in range(shards):
                out_ref[s, t * CHUNKS + c] = sums_ref[spans[s], c * LANES : (c + 1) * LANES]
    high, middle, low = pieces(stats)
    stats = jnp.where(lane < 2 * steps, high, jnp.where(lane < 4 * steps, middle, low))
    stats_ref[...] = stats.astype(bf16)
    for s in range(shards):
        out_ref[s, steps * CHUNKS] = stats_ref[spans[s], :]


def merge_kernel(parts_ref, value_ref, out_ref):
    shards, _, heads_dev, _ = parts_ref.shape
    steps = out_ref.shape[0]
    stats = parts_ref[:, steps * CHUNKS].astype(f32)
    latent_out = []
    for t in range(steps):
        peak, total = (
            stats[:, :, k : k + 1]
            + stats[:, :, k + 2 * steps : k + 2 * steps + 1]
            + stats[:, :, k + 4 * steps : k + 4 * steps + 1]
            for k in (2 * t, 2 * t + 1)
        )
        factor = jnp.exp(peak - jnp.max(peak, axis=0, keepdims=True))
        whole = jnp.sum(total * factor, axis=0)
        wide = jnp.broadcast_to(factor, (shards, heads_dev, LANES))
        chunks = []
        for c in range(CHUNKS):
            part = parts_ref[:, t * CHUNKS + c].astype(f32)
            chunks.append(jnp.sum(part * wide, axis=0) / whole)
        latent_out.append(jnp.concatenate(chunks, axis=1))
    latent_out = jnp.concatenate(latent_out, axis=0).astype(bf16)
    row = lax.broadcasted_iota(jnp.int32, (steps * heads_dev, LANES), 0) % heads_dev
    heads = jnp.zeros((steps * heads_dev, LANES), f32)
    for h in range(heads_dev):
        product = jnp.dot(latent_out, value_ref[h], preferred_element_type=f32)
        heads = jnp.where(row == h, product, heads)
    for t in range(steps):
        out_ref[t] = heads[t * heads_dev : (t + 1) * heads_dev, :].astype(bf16)


def merge_last_kernel(parts_ref, value_ref, *refs):
    *earlier_refs, out_ref, heads_ref = refs
    merge_kernel(parts_ref, value_ref, heads_ref)
    t = 0
    for done_ref in (*earlier_refs, heads_ref):
        for k in range(done_ref.shape[0]):
            mine = done_ref[k]
            out_ref[:, t] = jnp.broadcast_to(mine[None], (out_ref.shape[0], *mine.shape))
            t += 1


def pick_kernel(out_ref):
    heads_dev, width, rows = out_ref.shape
    queries = width // 2
    out_row = lax.broadcasted_iota(jnp.int32, (width, rows), 0)
    in_row = lax.broadcasted_iota(jnp.int32, (width, rows), 1)
    source = jnp.where(out_row < queries, out_row, out_row - queries) * heads_dev
    for h in range(heads_dev):
        out_ref[h] = jnp.where(in_row == source + h, 1.0, 0.0).astype(bf16)


def project_kernel(heads_ref, pick_ref, weight_ref, out_ref, flat_ref, wide_ref):
    requests, steps, heads_dev, _ = heads_ref.shape
    queries = requests * steps
    shards, half, width = out_ref.shape
    for q in range(queries):
        flat_ref[q * heads_dev : (q + 1) * heads_dev, :] = heads_ref[q // steps, q % steps]
    every = flat_ref[...]
    mixed = jnp.zeros(wide_ref.shape, f32)
    for h in range(heads_dev):
        of_head = jnp.dot(pick_ref[h], every, preferred_element_type=f32).astype(bf16)
        mixed = mixed + lax.dot_general(
            weight_ref[:, h * LANES : (h + 1) * LANES],
            of_head,
            (((1,), (1,)), ((), ())),
            preferred_element_type=f32,
        )
    wide_ref[...] = mixed
    lane = lax.broadcasted_iota(jnp.int32, (half, width), 1)
    for s in range(shards):
        first = wide_ref[2 * half * s : 2 * half * s + half, :]
        second = wide_ref[2 * half * s + half : 2 * half * (s + 1), :]
        out_ref[s] = jnp.where(lane < queries, first, second).astype(bf16)


def finish_kernel(parts_ref, out_ref):
    _, half, width = parts_ref.shape
    total = jnp.sum(parts_ref[...].astype(f32), axis=0)
    out_ref[:half, :] = total[:, : width // 2].astype(bf16)
    out_ref[half:, :] = total[:, width // 2 :].astype(bf16)


def exchanged(value, axis):
    return lax.all_to_all(value, axis, 0, 0, tiled=True)


def kernel(fn, shape, scratch=(), dtype=bf16):
    return pl.pallas_call(
        fn,
        out_shape=jax.ShapeDtypeStruct(shape, dtype),
        scratch_shapes=[pltpu.VMEM(*s) for s in scratch],
        compiler_params=pltpu.CompilerParams(vmem_limit_bytes=GRANT),
    )


def layer(latent_cache, queries, chosen, position, w_value, w_out):
    cache_len, key_width = latent_cache.shape[1:]
    _, steps, heads_dev, _ = queries.shape
    shards = lax.axis_size("seq")
    requests = lax.axis_size("req")
    heads = shards * heads_dev
    count = requests * steps

    counts = [end - begin for begin, end in STREAMS]
    query_all = pl.pallas_call(
        spread_kernel,
        out_shape=tuple(
            jax.ShapeDtypeStruct((shards, n * CHUNKS + (n + 1) // 2, heads_dev, LANES), bf16)
            for n in counts
        ),
        in_specs=[pl.BlockSpec(memory_space=pltpu.HBM)],
        scratch_shapes=[
            pltpu.VMEM((steps, heads_dev, key_width), bf16),
            pltpu.SemaphoreType.DMA(()),
        ],
        compiler_params=pltpu.CompilerParams(vmem_limit_bytes=GRANT),
        name="spread",
    )(pltpu.with_memory_space_constraint(queries[0], pltpu.HBM))
    query_all = [exchanged(value, "seq") for value in query_all]
    usable = pl.pallas_call(
        mark_kernel,
        out_shape=jax.ShapeDtypeStruct((steps, cache_len), f32),
        in_specs=[
            pl.BlockSpec(memory_space=pltpu.VMEM),
            pl.BlockSpec(memory_space=pltpu.SMEM),
        ],
        compiler_params=pltpu.CompilerParams(vmem_limit_bytes=GRANT),
        name="mark",
    )(jnp.swapaxes(chosen, 0, 1), position)
    pick = kernel(pick_kernel, (heads_dev, 2 * count, count * heads_dev))()
    usable, pick = lax.optimization_barrier((usable, pick))
    parts = []
    for k, n in enumerate(counts):
        part = kernel(
            functools.partial(attend_kernel, STREAMS[k][0]),
            (shards, n * CHUNKS + 1, heads_dev, LANES),
            (
                (((n + 1) // 2, heads, LANES), bf16),
                ((heads, LANES), bf16),
                *(((heads, LATENT), bf16),) * (2 * n),
            ),
        )(usable, query_all[k], latent_cache[0].T)
        parts.append(exchanged(part, "seq"))
    vdim = w_value.shape[2]
    merged = [
        kernel(merge_kernel, (n, heads_dev, vdim))(parts[k], w_value)
        for k, n in enumerate(counts[:-1])
    ]
    head_out = kernel(
        merge_last_kernel,
        (requests, steps, heads_dev, vdim),
        (((counts[-1], heads_dev, vdim), bf16),),
    )(parts[-1], w_value, *merged)
    head_out = exchanged(head_out, "req")
    features = w_out.shape[1]
    mixed = kernel(
        project_kernel,
        (shards, features // shards // 2, 2 * count),
        (((count * heads_dev, LANES), bf16), ((features, 2 * count), f32)),
    )(head_out, pick, w_out.T)
    mixed = exchanged(mixed, "seq")
    return kernel(finish_kernel, (features // shards, count))(mixed)


def solution(mesh):
    return jax.shard_map(
        layer,
        mesh=mesh,
        in_specs=(
            P("req", "seq", None),
            P("req", None, "seq", None),
            P("req", None, None),
            P("req"),
            P("seq", None, None),
            P("seq", "req"),
        ),
        out_specs=P(("req", "seq"), None),
        check_vma=False,
    )
```

time: 83.1 us -> 83.6 us (level)
  blocking collectives: 77.6 us -> 49.6 us
  starting transfers between devices: 0 us -> 13.8 us
  waiting for transfers between devices: 0 us -> 13.6 us
  Pallas kernels: 4.42 us -> 5.33 us
    all_to_all x4 -> x3, blocking collectives: 77.6 us -> 49.6 us  [exchanged(): return lax.all_to_all(value, axis, 0, 0, tiled=True)]
    all_to_all x0 -> x1, starting transfers between devices: none -> 13.8 us  [exchanged(): return lax.all_to_all(value, axis, 0, 0, tiled=True)]
    all_to_all x0 -> x1, waiting for transfers between devices: none -> 13.6 us  [exchanged(): return lax.all_to_all(value, axis, 0, 0, tiled=True)]
    pallas_call x5 -> x7, Pallas kernels: 4.42 us -> 5.33 us  [the longest x1 1.63 us: layer(): pl.pallas_call(spread_kernel, out_shape=tuple((jax.ShapeDtypeStruct((shar...]
  transfers between devices with their start and end apart: 0 -> 1, of which waited for: 0 -> 1; matrix products, arithmetic and copies ran while one was open for 0% -> 0% of each run, Pallas kernels for 0% -> 0%
where the time goes in v5:
time: 83.6 us; the launch traced here: 83.2 us
  blocking collectives  49.6 us (59%)
  starting transfers between devices  13.8 us (17%)
  waiting for transfers between devices  13.6 us (16%)
  Pallas kernels  5.33 us (6%)
    all_to_all x3, blocking collectives, exchanged(): return lax.all_to_all(value, axis, 0, 0, tiled=True)  49.6 us
    all_to_all x1, starting transfers between devices, exchanged(): return lax.all_to_all(value, axis, 0, 0, tiled=True)  13.8 us
    all_to_all x1, waiting for transfers between devices, exchanged(): return lax.all_to_all(value, axis, 0, 0, tiled=True)  13.6 us
  transfers between devices with their start and end apart: 1, of which 1 were waited for; matrix products, arithmetic and copies ran while one was open for 0% of the time, Pallas kernels for 0%

profile of v5, /device:TPU:1, one launch (start us, length us, event | category | flops | bytes accessed | tf_op | source)
XLA Modules:
  0.0 83.2 jit_solution(7083608566228944935)
XLA Ops:
  0.0 1.6 %spread.1 = bf16[32,14,4,128]{3,2,1,0:T(4,128)(2,1)} custom-call(bf16[3,4,576]{2,1,0:T(4,128)(2,1)} %bitcast.9), custom_call_target="tpu_custom_call" | custom-call | tf_op jit(solution)/shard_map/spread/pallas_call | solution.py:212
  1.6 0.0 copy-start
  1.7 13.8 %all-to-all-start = ((bf16[32,14,4,128]{3,2,1,0:T(4,128)(2,1)}), bf16[32,14,4,128]{3,2,1,0:T(4,128)(2,1)S(1)}, u32[]{:S(2)}, u32[]{:S(2)}) async-start(bf16[32,14,4,128]{3,2,1,0:T(4,128)(2,1)} %spread.1), calls=%async_computation | async-start | bytes 917504 | tf_op jit(solution)/shard_map/all_to_all | solution.py:191
  15.6 0.0 copy-start.3
  16.2 0.0 copy-done.3
  16.2 0.1 mark.1.usable_ref
  16.4 13.6 %all-to-all-done.query_ref = bf16[32,14,4,128]{3,2,1,0:T(4,128)(2,1)S(1)} async-done(((bf16[32,14,4,128]{3,2,1,0:T(4,128)(2,1)}), bf16[32,14,4,128]{3,2,1,0:T(4,128)(2,1)S(1)}, u32[]{:S(2)}, u32[]{:S(2)}) %all-to-all-start) | async-done | bytes 458784 | tf_op jit(solution)/shard_map/all_to_all | solution.py:191
  30.0 0.0 copy-done
  30.0 1.5 %shard_map.65 = bf16[32,13,4,128]{3,2,1,0:T(4,128)(2,1)S(1)} custom-call(f32[3,512]{1,0:T(4,128)S(1)} %mark.1.usable_ref, bf16[32,14,4,128]{3,2,1,0:T(4,128)(2,1)S(1)} %all-to-all-done.query_ref, bf16[576,512]{1,0:T(8,128)(2,1)S(1)} %bitcast.6), custom_call_target="tpu_custom_call" | custom-call | tf_op jit(solution)/shard_map/pallas_call | solution.py:241
  31.4 0.0 copy-start.1
  31.5 19.2 %all_to_all.20.parts_ref = bf16[32,13,4,128]{3,2,1,0:T(4,128)(2,1)S(1)} all-to-all(bf16[32,13,4,128]{3,2,1,0:T(4,128)(2,1)S(1)} %shard_map.65), channel_id=1, replica_groups=mesh['req'=16,'seq'=32] {'seq'}, dimensions={0} | all-to-all | bytes 851968 | tf_op jit(solution)/shard_map/all_to_all | solution.py:191
  50.6 0.0 copy-done.1
  50.6 0.0 copy-start.2
  50.6 0.7 shard_map.66
  51.3 17.9 %all_to_all.21.heads_ref = bf16[16,3,4,128]{3,2,1,0:T(4,128)(2,1)S(1)} all-to-all(bf16[16,3,4,128]{3,2,1,0:T(4,128)(2,1)S(1)} %shard_map.66), channel_id=1, replica_groups=mesh['req'=16,'seq'=32] {'req'}, dimensions={0} | all-to-all | bytes 98304 | tf_op jit(solution)/shard_map/all_to_all | solution.py:191
  69.2 0.0 copy-done.2
  69.2 0.7 shard_map.67
  69.9 12.6 %all_to_all.22.parts_ref = bf16[32,7,96]{2,1,0:T(8,128)(2,1)S(1)} all-to-all(bf16[32,7,96]{2,1,0:T(8,128)(2,1)S(1)} %shard_map.67), channel_id=1, replica_groups=mesh['req'=16,'seq'=32] {'seq'}, dimensions={0} | all-to-all | bytes 86016 | tf_op jit(solution)/shard_map/all_to_all | solution.py:191
  82.5 0.7 shard_map.68
  (1 shorter events, 0.0 us)
Async XLA Ops:
  1.6 28.3 %copy-start = (bf16[1,512,576]{1,2,0:T(8,128)(2,1)S(1)}, bf16[1,512,576]{1,2,0:T(8,128)(2,1)}, u32[]{:S(2)}) copy-start(bf16[1,512,576]{1,2,0:T(8,128)(2,1)} %param.6) | copy-start | bytes 1769476
  1.7 28.3 %all-to-all-start = ((bf16[32,14,4,128]{3,2,1,0:T(4,128)(2,1)}), bf16[32,14,4,128]{3,2,1,0:T(4,128)(2,1)S(1)}, u32[]{:S(2)}, u32[]{:S(2)}) async-start(bf16[32,14,4,128]{3,2,1,0:T(4,128)(2,1)} %spread.1), calls=%async_computation | async-start | bytes 917504 | tf_op jit(solution)/shard_map/all_to_all | solution.py:191
  15.6 0.7 copy-start.3
  31.4 19.2 %copy-start.1 = (bf16[4,512,128]{2,1,0:T(8,128)(2,1)S(1)}, bf16[4,512,128]{2,1,0:T(8,128)(2,1)}, u32[]{:S(2)}) copy-start(bf16[4,512,128]{2,1,0:T(8,128)(2,1)} %value_ref.1) | copy-start | bytes 1572868
  50.6 18.6 %copy-start.2 = (bf16[512,448]{0,1:T(8,128)(2,1)S(1)}, bf16[512,448]{0,1:T(8,128)(2,1)}, u32[]{:S(2)}) copy-start(bf16[512,448]{0,1:T(8,128)(2,1)} %param.11) | copy-start | bytes 1376260

commit v6 on v4

--- a/solution.py
+++ b/solution.py
@@ -13,6 +13,7 @@
 LANES = 128
 CHUNKS = LATENT // LANES
 GRANT = 12 * 1024 * 1024
+LAG_NS = 3000
 
 score_scale = 1.0 / math.sqrt(192.0)
 very_low = -1e30
@@ -63,6 +64,10 @@
         named = jnp.where(chosen_ref[t] == block, 1.0, 0.0)
         named = jnp.max(named, axis=1, keepdims=True)
         usable_ref[t : t + 1, :] = jnp.max(jnp.where(mine, named, 0.0), axis=0, keepdims=True)
+
+    @pl.when(lax.axis_index("req") % 2 == 0)
+    def _():
+        pl.delay(LAG_NS)
 
 
 def attend_kernel(usable_ref, query_ref, cache_ref, out_ref, rotary_ref, stats_ref, *work):

time: 83.1 us -> 80.7 us (0.971)
  blocking collectives: 77.6 us -> 75.1 us
    all_to_all x4, blocking collectives: 77.6 us -> 75.1 us  [exchanged(): return lax.all_to_all(value, axis, 0, 0, tiled=True)]
where the time goes in v6:
time: 80.7 us; the launch traced here: 80.3 us
  blocking collectives  75.1 us (93%)
  Pallas kernels  4.42 us (5%)
    all_to_all x4, blocking collectives, exchanged(): return lax.all_to_all(value, axis, 0, 0, tiled=True)  75.1 us

profile of v6, /device:TPU:1, one launch (start us, length us, event | category | flops | bytes accessed | tf_op | source)
XLA Modules:
  0.0 80.3 jit_solution(11067674742344832046)
XLA Ops:
  0.0 0.0 copy-start
  0.7 0.9 %spread.1 = (bf16[32,56,128]{2,1,0:T(8,128)(2,1)S(1)}, f32[3,512]{1,0:T(4,128)S(1)}) custom-call(bf16[3,4,576]{2,1,0:T(4,128)(2,1)} %bitcast.8, s32[3,1,32]{2,1,0:T(1,128)} %bitcast.9, s32[1]{0:T(128)S(6)} %copy.7.position_ref), custom_call_target="tpu_custom_call" | custom-call | tf_op jit(solution)/shard_map/spread/pallas_call | solution.py:204
  1.6 25.8 %all_to_all.20.query_ref = bf16[32,56,128]{2,1,0:T(8,128)(2,1)S(1)} all-to-all(bf16[32,56,128]{2,1,0:T(8,128)(2,1)S(1)} %get-tuple-element.8), channel_id=1, replica_groups=mesh['req'=16,'seq'=32] {'seq'}, dimensions={0} | all-to-all | bytes 917504 | tf_op jit(solution)/shard_map/all_to_all | solution.py:183
  27.4 0.0 copy-done
  27.4 1.5 %attend.1 = bf16[32,13,4,128]{3,2,1,0:T(4,128)(2,1)S(1)} custom-call(f32[3,512]{1,0:T(4,128)S(1)} %get-tuple-element.7.usable_ref, bf16[32,56,128]{2,1,0:T(8,128)(2,1)S(1)} %all_to_all.20.query_ref, bf16[576,512]{1,0:T(8,128)(2,1)S(1)} %bitcast.6), custom_call_target="tpu_custom_call" | custom-call | tf_op jit(solution)/shard_map/attend/pallas_call | solution.py:225
  28.9 0.0 copy-start.1
  28.9 16.9 %all_to_all.21.parts_ref = bf16[32,13,4,128]{3,2,1,0:T(4,128)(2,1)S(1)} all-to-all(bf16[32,13,4,128]{3,2,1,0:T(4,128)(2,1)S(1)} %attend.1), channel_id=1, replica_groups=mesh['req'=16,'seq'=32] {'seq'}, dimensions={0} | all-to-all | bytes 851968 | tf_op jit(solution)/shard_map/all_to_all | solution.py:183
  45.8 0.0 copy-done.1
  45.8 0.0 copy-start.2
  45.8 0.7 merge.1
  46.5 20.2 %all_to_all.22.heads_ref = bf16[16,3,4,128]{3,2,1,0:T(4,128)(2,1)S(1)} all-to-all(bf16[16,3,4,128]{3,2,1,0:T(4,128)(2,1)S(1)} %merge.1), channel_id=1, replica_groups=mesh['req'=16,'seq'=32] {'req'}, dimensions={0} | all-to-all | bytes 98304 | tf_op jit(solution)/shard_map/all_to_all | solution.py:183
  66.7 0.0 copy-done.2
  66.7 0.7 project.1
  67.4 12.2 %all_to_all.23.parts_ref = bf16[32,7,96]{2,1,0:T(8,128)(2,1)S(1)} all-to-all(bf16[32,7,96]{2,1,0:T(8,128)(2,1)S(1)} %project.1), channel_id=1, replica_groups=mesh['req'=16,'seq'=32] {'seq'}, dimensions={0} | all-to-all | bytes 86016 | tf_op jit(solution)/shard_map/all_to_all | solution.py:183
  79.6 0.7 finish.1
Async XLA Ops:
  0.0 27.4 %copy-start = (bf16[1,512,576]{1,2,0:T(8,128)(2,1)S(1)}, bf16[1,512,576]{1,2,0:T(8,128)(2,1)}, u32[]{:S(2)}) copy-start(bf16[1,512,576]{1,2,0:T(8,128)(2,1)} %param.6) | copy-start | bytes 1769476
  28.9 16.9 %copy-start.1 = (bf16[4,512,128]{2,1,0:T(8,128)(2,1)S(1)}, bf16[4,512,128]{2,1,0:T(8,128)(2,1)}, u32[]{:S(2)}) copy-start(bf16[4,512,128]{2,1,0:T(8,128)(2,1)} %value_ref.1) | copy-start | bytes 1572868
  45.8 20.9 %copy-start.2 = (bf16[512,448]{0,1:T(8,128)(2,1)S(1)}, bf16[512,448]{0,1:T(8,128)(2,1)}, u32[]{:S(2)}) copy-start(bf16[512,448]{0,1:T(8,128)(2,1)} %param.11) | copy-start | bytes 1376260

commit v7 on v6

--- a/solution.py
+++ b/solution.py
@@ -70,47 +70,58 @@
         pl.delay(LAG_NS)
 
 
-def attend_kernel(usable_ref, query_ref, cache_ref, out_ref, rotary_ref, stats_ref, *work):
+def attend_kernel(usable_ref, query_ref, cache_ref, out_ref, rows_ref, rotary_ref, sums_ref, stats_ref):
     shards = query_ref.shape[0]
     steps = usable_ref.shape[0]
     heads = rotary_ref.shape[1]
     heads_dev = heads // shards
-    spans = [slice(s * heads_dev, (s + 1) * heads_dev) for s in range(shards)]
     for pair in range(rotary_ref.shape[0]):
         k = (steps * CHUNKS + pair) * heads_dev
         for s in range(shards):
-            rotary_ref[pair, spans[s], :] = query_ref[s, k : k + heads_dev, :]
-    latent = cache_ref[:LATENT, :]
-    rotary_keys = cache_ref[LATENT:, :]
+            rotary_ref[pair, s * heads_dev : (s + 1) * heads_dev, :] = query_ref[s, k : k + heads_dev, :]
+    for t in range(steps):
+        for c in range(CHUNKS):
+            k = (t * CHUNKS + c) * heads_dev
+            for s in range(shards):
+                row = t * heads + s * heads_dev
+                rows_ref[row : row + heads_dev, c * LANES : (c + 1) * LANES] = query_ref[
+                    s, k : k + heads_dev, :
+                ]
+    rotary = jnp.concatenate(
+        [rotary_ref[t // 2, :, (t % 2) * ROPE : (t % 2 + 1) * ROPE] for t in range(steps)], axis=0
+    )
+    every = jnp.dot(rows_ref[...], cache_ref[:LATENT, :], preferred_element_type=f32)
+    every = every + jnp.dot(rotary, cache_ref[LATENT:, :], preferred_element_type=f32)
     lane = lax.broadcasted_iota(jnp.int32, (heads, LANES), 1)
     slot = lane % (2 * steps)
     stats = jnp.zeros((heads, LANES), f32)
-    for t in range(steps):
-        rows_ref, sums_ref = work[2 * t], work[2 * t + 1]
-        for c in range(CHUNKS):
-            k = (t * CHUNKS + c) * heads_dev
-            for s in range(shards):
-                rows_ref[spans[s], c * LANES : (c + 1) * LANES] = query_ref[s, k : k + heads_dev, :]
-        rotary = rotary_ref[t // 2, :, (t % 2) * ROPE : (t % 2 + 1) * ROPE]
-        scores = jnp.dot(rows_ref[...], latent, preferred_element_type=f32)
-        scores = scores + jnp.dot(rotary, rotary_keys, preferred_element_type=f32)
+    weights = []
+    for t in range(steps):
+        scores = every[t * heads : (t + 1) * heads]
         scores = jnp.where(usable_ref[t : t + 1, :] > 0.0, scores, very_low)
         peak = jnp.max(scores, axis=1, keepdims=True)
         raw = jnp.exp2((scores - peak) * (score_scale * math.log2(math.e)))
         total = jnp.sum(raw, axis=1, keepdims=True)
-        sums_ref[...] = lax.dot_general(
-            raw.astype(bf16), latent, (((1,), (1,)), ((), ())), preferred_element_type=f32
-        ).astype(bf16)
+        weights.append(raw.astype(bf16))
         stats = jnp.where(slot == 2 * t, peak * score_scale, stats)
         stats = jnp.where(slot == 2 * t + 1, total, stats)
-        for c in range(CHUNKS):
-            for s in range(shards):
-                out_ref[s, t * CHUNKS + c] = sums_ref[spans[s], c * LANES : (c + 1) * LANES]
+    sums_ref[...] = lax.dot_general(
+        jnp.concatenate(weights, axis=0),
+        cache_ref[:LATENT, :],
+        (((1,), (1,)), ((), ())),
+        preferred_element_type=f32,
+    ).astype(bf16)
     high, middle, low = pieces(stats)
     stats = jnp.where(lane < 2 * steps, high, jnp.where(lane < 4 * steps, middle, low))
     stats_ref[...] = stats.astype(bf16)
     for s in range(shards):
-        out_ref[s, steps * CHUNKS] = stats_ref[spans[s], :]
+        for t in range(steps):
+            row = t * heads + s * heads_dev
+            for c in range(CHUNKS):
+                out_ref[s, t * CHUNKS + c] = sums_ref[
+                    row : row + heads_dev, c * LANES : (c + 1) * LANES
+                ]
+        out_ref[s, steps * CHUNKS] = stats_ref[s * heads_dev : (s + 1) * heads_dev, :]
 
 
 def merge_kernel(parts_ref, value_ref, out_ref):
@@ -154,17 +165,16 @@
     out_row = lax.broadcasted_iota(jnp.int32, (width, queries * heads_dev), 0)
     in_row = lax.broadcasted_iota(jnp.int32, (width, queries * heads_dev), 1)
     source = jnp.where(out_row < queries, out_row, out_row - queries) * heads_dev
-    mixed = jnp.zeros(wide_ref.shape, f32)
+    of_heads = []
     for h in range(heads_dev):
         pick = jnp.where(in_row == source + h, 1.0, 0.0).astype(bf16)
-        of_head = jnp.dot(pick, every, preferred_element_type=f32).astype(bf16)
-        mixed = mixed + lax.dot_general(
-            weight_ref[:, h * LANES : (h + 1) * LANES],
-            of_head,
-            (((1,), (1,)), ((), ())),
-            preferred_element_type=f32,
-        )
-    wide_ref[...] = mixed
+        of_heads.append(jnp.dot(pick, every, preferred_element_type=f32).astype(bf16))
+    wide_ref[...] = lax.dot_general(
+        weight_ref[...],
+        jnp.concatenate(of_heads, axis=1),
+        (((1,), (1,)), ((), ())),
+        preferred_element_type=f32,
+    )
     lane = lax.broadcasted_iota(jnp.int32, (half, width), 1)
     for s in range(shards):
         first = wide_ref[2 * half * s : 2 * half * s + half, :]
@@ -227,9 +237,10 @@
         (shards, steps * CHUNKS + 1, heads_dev, LANES),
         "attend",
         (
+            ((steps * heads, LATENT), bf16),
             (((steps + 1) // 2, heads, LANES), bf16),
+            ((steps * heads, LATENT), bf16),
             ((heads, LANES), bf16),
-            *(((heads, LATENT), bf16),) * (2 * steps),
         ),
     )(usable, query_all, latent_cache[0].T)
     parts = exchanged(parts, "seq")

time: 80.7 us -> 80 us (level)
  no operation moved by 1% of the time
where the time goes in v7:
time: 80 us; the launch traced here: 79.7 us
  blocking collectives  75.1 us (94%)
  Pallas kernels  3.75 us (5%)
    all_to_all x4, blocking collectives, exchanged(): return lax.all_to_all(value, axis, 0, 0, tiled=True)  75.1 us

profile of v7, /device:TPU:1, one launch (start us, length us, event | category | flops | bytes accessed | tf_op | source)
XLA Modules:
  0.0 79.7 jit_solution(15487750396371747969)
XLA Ops:
  0.0 0.0 copy-start
  0.7 0.9 %spread.1 = (bf16[32,56,128]{2,1,0:T(8,128)(2,1)S(1)}, f32[3,512]{1,0:T(4,128)S(1)}) custom-call(bf16[3,4,576]{2,1,0:T(4,128)(2,1)} %bitcast.8, s32[3,1,32]{2,1,0:T(1,128)} %bitcast.9, s32[1]{0:T(128)S(6)} %copy.7.position_ref), custom_call_target="tpu_custom_call" | custom-call | tf_op jit(solution)/shard_map/spread/pallas_call | solution.py:214
  1.6 25.8 %all_to_all.20.query_ref = bf16[32,56,128]{2,1,0:T(8,128)(2,1)S(1)} all-to-all(bf16[32,56,128]{2,1,0:T(8,128)(2,1)S(1)} %get-tuple-element.8), channel_id=1, replica_groups=mesh['req'=16,'seq'=32] {'seq'}, dimensions={0} | all-to-all | bytes 917504 | tf_op jit(solution)/shard_map/all_to_all | solution.py:193
  27.4 0.0 copy-done
  27.4 1.0 %attend.1 = bf16[32,13,4,128]{3,2,1,0:T(4,128)(2,1)S(1)} custom-call(f32[3,512]{1,0:T(4,128)S(1)} %get-tuple-element.7.usable_ref, bf16[32,56,128]{2,1,0:T(8,128)(2,1)S(1)} %all_to_all.20.query_ref, bf16[576,512]{1,0:T(8,128)(2,1)S(1)} %bitcast.6), custom_call_target="tpu_custom_call" | custom-call | tf_op jit(solution)/shard_map/attend/pallas_call | solution.py:235
  28.4 0.0 copy-start.1
  28.4 16.9 %all_to_all.21.parts_ref = bf16[32,13,4,128]{3,2,1,0:T(4,128)(2,1)S(1)} all-to-all(bf16[32,13,4,128]{3,2,1,0:T(4,128)(2,1)S(1)} %attend.1), channel_id=1, replica_groups=mesh['req'=16,'seq'=32] {'seq'}, dimensions={0} | all-to-all | bytes 851968 | tf_op jit(solution)/shard_map/all_to_all | solution.py:193
  45.3 0.0 copy-done.1
  45.3 0.0 copy-start.2
  45.3 0.7 merge.1
  46.0 20.2 %all_to_all.22.heads_ref = bf16[16,3,4,128]{3,2,1,0:T(4,128)(2,1)S(1)} all-to-all(bf16[16,3,4,128]{3,2,1,0:T(4,128)(2,1)S(1)} %merge.1), channel_id=1, replica_groups=mesh['req'=16,'seq'=32] {'req'}, dimensions={0} | all-to-all | bytes 98304 | tf_op jit(solution)/shard_map/all_to_all | solution.py:193
  66.2 0.0 copy-done.2
  66.2 0.5 project.1
  66.8 12.2 %all_to_all.23.parts_ref = bf16[32,7,96]{2,1,0:T(8,128)(2,1)S(1)} all-to-all(bf16[32,7,96]{2,1,0:T(8,128)(2,1)S(1)} %project.1), channel_id=1, replica_groups=mesh['req'=16,'seq'=32] {'seq'}, dimensions={0} | all-to-all | bytes 86016 | tf_op jit(solution)/shard_map/all_to_all | solution.py:193
  79.0 0.7 finish.1
Async XLA Ops:
  0.0 27.4 %copy-start = (bf16[1,512,576]{1,2,0:T(8,128)(2,1)S(1)}, bf16[1,512,576]{1,2,0:T(8,128)(2,1)}, u32[]{:S(2)}) copy-start(bf16[1,512,576]{1,2,0:T(8,128)(2,1)} %param.6) | copy-start | bytes 1769476
  28.4 16.9 %copy-start.1 = (bf16[4,512,128]{2,1,0:T(8,128)(2,1)S(1)}, bf16[4,512,128]{2,1,0:T(8,128)(2,1)}, u32[]{:S(2)}) copy-start(bf16[4,512,128]{2,1,0:T(8,128)(2,1)} %value_ref.1) | copy-start | bytes 1572868
  45.3 20.9 %copy-start.2 = (bf16[512,448]{0,1:T(8,128)(2,1)S(1)}, bf16[512,448]{0,1:T(8,128)(2,1)}, u32[]{:S(2)}) copy-start(bf16[512,448]{0,1:T(8,128)(2,1)} %param.11) | copy-start | bytes 1376260

commit v8 on v7

--- a/solution.py
+++ b/solution.py
@@ -48,9 +48,10 @@
     rotary.append(jnp.zeros_like(rotary[0]))
     for t in range(0, len(rotary), 2):
         packed.append(jnp.concatenate([rotary[t], rotary[t + 1]], axis=1))
-    for k, piece in enumerate(packed):
-        out_ref[:, k * heads_dev : (k + 1) * heads_dev, :] = jnp.broadcast_to(
-            piece[None], (out_ref.shape[0], heads_dev, LANES)
+    for k in range(0, len(packed), 2):
+        tile = jnp.concatenate(packed[k : k + 2], axis=0)
+        out_ref[:, k * heads_dev : (k + 2) * heads_dev, :] = jnp.broadcast_to(
+            tile[None], (out_ref.shape[0], *tile.shape)
         )
     cache_len = usable_ref.shape[1]
     blocks = cache_len // BLOCK
@@ -128,17 +129,17 @@
     shards, _, heads_dev, _ = parts_ref.shape
     requests, steps, _, _ = out_ref.shape
     stats = parts_ref[:, steps * CHUNKS].astype(f32)
+
+    def shifted(value, by):
+        return pltpu.roll(value, LANES - by, 2)
+
+    stats = stats + shifted(stats, 2 * steps) + shifted(stats, 4 * steps)
+    factors = jnp.exp(stats - jnp.max(stats, axis=0, keepdims=True))
+    wholes = jnp.sum(shifted(stats, 1) * factors, axis=0)
     latent_out = []
     for t in range(steps):
-        peak, total = (
-            stats[:, :, k : k + 1]
-            + stats[:, :, k + 2 * steps : k + 2 * steps + 1]
-            + stats[:, :, k + 4 * steps : k + 4 * steps + 1]
-            for k in (2 * t, 2 * t + 1)
-        )
-        factor = jnp.exp(peak - jnp.max(peak, axis=0, keepdims=True))
-        whole = jnp.sum(total * factor, axis=0)
-        wide = jnp.broadcast_to(factor, (shards, heads_dev, LANES))
+        whole = wholes[:, 2 * t : 2 * t + 1]
+        wide = jnp.broadcast_to(factors[:, :, 2 * t : 2 * t + 1], (shards, heads_dev, LANES))
         chunks = []
         for c in range(CHUNKS):
             part = parts_ref[:, t * CHUNKS + c].astype(f32)
@@ -146,10 +147,14 @@
         latent_out.append(jnp.concatenate(chunks, axis=1))
     latent_out = jnp.concatenate(latent_out, axis=0).astype(bf16)
     row = lax.broadcasted_iota(jnp.int32, (steps * heads_dev, LANES), 0) % heads_dev
-    heads = jnp.zeros((steps * heads_dev, LANES), f32)
-    for h in range(heads_dev):
-        product = jnp.dot(latent_out, value_ref[h], preferred_element_type=f32)
-        heads = jnp.where(row == h, product, heads)
+    every = jnp.dot(
+        latent_out,
+        jnp.concatenate([value_ref[h] for h in range(heads_dev)], axis=1),
+        preferred_element_type=f32,
+    )
+    heads = every[:, :LANES]
+    for h in range(1, heads_dev):
+        heads = jnp.where(row == h, every[:, h * LANES : (h + 1) * LANES], heads)
     for t in range(steps):
         mine = heads[t * heads_dev : (t + 1) * heads_dev, :].astype(bf16)
         out_ref[:, t] = jnp.broadcast_to(mine[None], (requests, heads_dev, LANES))

time: 80 us -> 79.8 us (level)
  no operation moved by 1% of the time
where the time goes in v8:
time: 79.8 us; the launch traced here: 79.5 us
  blocking collectives  75.1 us (94%)
  Pallas kernels  3.58 us (4%)
    all_to_all x4, blocking collectives, exchanged(): return lax.all_to_all(value, axis, 0, 0, tiled=True)  75.1 us

profile of v8, /device:TPU:1, one launch (start us, length us, event | category | flops | bytes accessed | tf_op | source)
XLA Modules:
  0.0 79.5 jit_solution(17239034254190417554)
XLA Ops:
  0.0 0.0 copy-start
  0.7 0.8 %spread.1 = (bf16[32,56,128]{2,1,0:T(8,128)(2,1)S(1)}, f32[3,512]{1,0:T(4,128)S(1)}) custom-call(bf16[3,4,576]{2,1,0:T(4,128)(2,1)} %bitcast.8, s32[3,1,32]{2,1,0:T(1,128)} %bitcast.9, s32[1]{0:T(128)S(6)} %copy.7.position_ref), custom_call_target="tpu_custom_call" | custom-call | tf_op jit(solution)/shard_map/spread/pallas_call | solution.py:219
  1.6 25.8 %all_to_all.20.query_ref = bf16[32,56,128]{2,1,0:T(8,128)(2,1)S(1)} all-to-all(bf16[32,56,128]{2,1,0:T(8,128)(2,1)S(1)} %get-tuple-element.8), channel_id=1, replica_groups=mesh['req'=16,'seq'=32] {'seq'}, dimensions={0} | all-to-all | bytes 917504 | tf_op jit(solution)/shard_map/all_to_all | solution.py:198
  27.4 0.0 copy-done
  27.4 1.0 %attend.1 = bf16[32,13,4,128]{3,2,1,0:T(4,128)(2,1)S(1)} custom-call(f32[3,512]{1,0:T(4,128)S(1)} %get-tuple-element.7.usable_ref, bf16[32,56,128]{2,1,0:T(8,128)(2,1)S(1)} %all_to_all.20.query_ref, bf16[576,512]{1,0:T(8,128)(2,1)S(1)} %bitcast.6), custom_call_target="tpu_custom_call" | custom-call | tf_op jit(solution)/shard_map/attend/pallas_call | solution.py:240
  28.4 0.0 copy-start.1
  28.4 16.9 %all_to_all.21.parts_ref = bf16[32,13,4,128]{3,2,1,0:T(4,128)(2,1)S(1)} all-to-all(bf16[32,13,4,128]{3,2,1,0:T(4,128)(2,1)S(1)} %attend.1), channel_id=1, replica_groups=mesh['req'=16,'seq'=32] {'seq'}, dimensions={0} | all-to-all | bytes 851968 | tf_op jit(solution)/shard_map/all_to_all | solution.py:198
  45.3 0.0 copy-done.1
  45.3 0.0 copy-start.2
  45.3 0.6 merge.1
  45.9 20.2 %all_to_all.22.heads_ref = bf16[16,3,4,128]{3,2,1,0:T(4,128)(2,1)S(1)} all-to-all(bf16[16,3,4,128]{3,2,1,0:T(4,128)(2,1)S(1)} %merge.1), channel_id=1, replica_groups=mesh['req'=16,'seq'=32] {'req'}, dimensions={0} | all-to-all | bytes 98304 | tf_op jit(solution)/shard_map/all_to_all | solution.py:198
  66.1 0.0 copy-done.2
  66.1 0.5 project.1
  66.6 12.2 %all_to_all.23.parts_ref = bf16[32,7,96]{2,1,0:T(8,128)(2,1)S(1)} all-to-all(bf16[32,7,96]{2,1,0:T(8,128)(2,1)S(1)} %project.1), channel_id=1, replica_groups=mesh['req'=16,'seq'=32] {'seq'}, dimensions={0} | all-to-all | bytes 86016 | tf_op jit(solution)/shard_map/all_to_all | solution.py:198
  78.8 0.7 finish.1
Async XLA Ops:
  0.0 27.4 %copy-start = (bf16[1,512,576]{1,2,0:T(8,128)(2,1)S(1)}, bf16[1,512,576]{1,2,0:T(8,128)(2,1)}, u32[]{:S(2)}) copy-start(bf16[1,512,576]{1,2,0:T(8,128)(2,1)} %param.6) | copy-start | bytes 1769476
  28.4 16.9 %copy-start.1 = (bf16[4,512,128]{2,1,0:T(8,128)(2,1)S(1)}, bf16[4,512,128]{2,1,0:T(8,128)(2,1)}, u32[]{:S(2)}) copy-start(bf16[4,512,128]{2,1,0:T(8,128)(2,1)} %value_ref.1) | copy-start | bytes 1572868
  45.3 20.8 %copy-start.2 = (bf16[512,448]{0,1:T(8,128)(2,1)S(1)}, bf16[512,448]{0,1:T(8,128)(2,1)}, u32[]{:S(2)}) copy-start(bf16[512,448]{0,1:T(8,128)(2,1)} %param.11) | copy-start | bytes 1376260

commit v9 on v8

--- a/solution.py
+++ b/solution.py
@@ -13,7 +13,7 @@
 LANES = 128
 CHUNKS = LATENT // LANES
 GRANT = 12 * 1024 * 1024
-LAG_NS = 3000
+LAG_NS = 2000
 
 score_scale = 1.0 / math.sqrt(192.0)
 very_low = -1e30

time: 79.8 us -> 80.9 us (1.014)
  blocking collectives: 75.1 us -> 76.2 us
    all_to_all x4, blocking collectives: 75.1 us -> 76.2 us  [exchanged(): return lax.all_to_all(value, axis, 0, 0, tiled=True)]
where the time goes in v9:
time: 80.9 us; the launch traced here: 80.5 us
  blocking collectives  76.2 us (94%)
  Pallas kernels  3.59 us (4%)
    all_to_all x4, blocking collectives, exchanged(): return lax.all_to_all(value, axis, 0, 0, tiled=True)  76.2 us

profile of v9, /device:TPU:1, one launch (start us, length us, event | category | flops | bytes accessed | tf_op | source)
XLA Modules:
  0.0 80.5 jit_solution(11405046274579715396)
XLA Ops:
  0.0 0.0 copy-start
  0.7 0.8 %spread.1 = (bf16[32,56,128]{2,1,0:T(8,128)(2,1)S(1)}, f32[3,512]{1,0:T(4,128)S(1)}) custom-call(bf16[3,4,576]{2,1,0:T(4,128)(2,1)} %bitcast.8, s32[3,1,32]{2,1,0:T(1,128)} %bitcast.9, s32[1]{0:T(128)S(6)} %copy.7.position_ref), custom_call_target="tpu_custom_call" | custom-call | tf_op jit(solution)/shard_map/spread/pallas_call | solution.py:219
  1.6 26.1 %all_to_all.20.query_ref = bf16[32,56,128]{2,1,0:T(8,128)(2,1)S(1)} all-to-all(bf16[32,56,128]{2,1,0:T(8,128)(2,1)S(1)} %get-tuple-element.8), channel_id=1, replica_groups=mesh['req'=16,'seq'=32] {'seq'}, dimensions={0} | all-to-all | bytes 917504 | tf_op jit(solution)/shard_map/all_to_all | solution.py:198
  27.7 0.0 copy-done
  27.7 1.0 %attend.1 = bf16[32,13,4,128]{3,2,1,0:T(4,128)(2,1)S(1)} custom-call(f32[3,512]{1,0:T(4,128)S(1)} %get-tuple-element.7.usable_ref, bf16[32,56,128]{2,1,0:T(8,128)(2,1)S(1)} %all_to_all.20.query_ref, bf16[576,512]{1,0:T(8,128)(2,1)S(1)} %bitcast.6), custom_call_target="tpu_custom_call" | custom-call | tf_op jit(solution)/shard_map/attend/pallas_call | solution.py:240
  28.6 0.0 copy-start.1
  28.7 17.8 %all_to_all.21.parts_ref = bf16[32,13,4,128]{3,2,1,0:T(4,128)(2,1)S(1)} all-to-all(bf16[32,13,4,128]{3,2,1,0:T(4,128)(2,1)S(1)} %attend.1), channel_id=1, replica_groups=mesh['req'=16,'seq'=32] {'seq'}, dimensions={0} | all-to-all | bytes 851968 | tf_op jit(solution)/shard_map/all_to_all | solution.py:198
  46.5 0.0 copy-done.1
  46.5 0.0 copy-start.2
  46.5 0.6 merge.1
  47.1 20.0 %all_to_all.22.heads_ref = bf16[16,3,4,128]{3,2,1,0:T(4,128)(2,1)S(1)} all-to-all(bf16[16,3,4,128]{3,2,1,0:T(4,128)(2,1)S(1)} %merge.1), channel_id=1, replica_groups=mesh['req'=16,'seq'=32] {'req'}, dimensions={0} | all-to-all | bytes 98304 | tf_op jit(solution)/shard_map/all_to_all | solution.py:198
  67.1 0.0 copy-done.2
  67.1 0.5 project.1
  67.6 12.2 %all_to_all.23.parts_ref = bf16[32,7,96]{2,1,0:T(8,128)(2,1)S(1)} all-to-all(bf16[32,7,96]{2,1,0:T(8,128)(2,1)S(1)} %project.1), channel_id=1, replica_groups=mesh['req'=16,'seq'=32] {'seq'}, dimensions={0} | all-to-all | bytes 86016 | tf_op jit(solution)/shard_map/all_to_all | solution.py:198
  79.8 0.7 finish.1
Async XLA Ops:
  0.0 27.7 %copy-start = (bf16[1,512,576]{1,2,0:T(8,128)(2,1)S(1)}, bf16[1,512,576]{1,2,0:T(8,128)(2,1)}, u32[]{:S(2)}) copy-start(bf16[1,512,576]{1,2,0:T(8,128)(2,1)} %param.6) | copy-start | bytes 1769476
  28.6 17.9 %copy-start.1 = (bf16[4,512,128]{2,1,0:T(8,128)(2,1)S(1)}, bf16[4,512,128]{2,1,0:T(8,128)(2,1)}, u32[]{:S(2)}) copy-start(bf16[4,512,128]{2,1,0:T(8,128)(2,1)} %value_ref.1) | copy-start | bytes 1572868
  46.5 20.6 %copy-start.2 = (bf16[512,448]{0,1:T(8,128)(2,1)S(1)}, bf16[512,448]{0,1:T(8,128)(2,1)}, u32[]{:S(2)}) copy-start(bf16[512,448]{0,1:T(8,128)(2,1)} %param.11) | copy-start | bytes 1376260

commit v10 on v9

--- a/solution.py
+++ b/solution.py
@@ -13,7 +13,7 @@
 LANES = 128
 CHUNKS = LATENT // LANES
 GRANT = 12 * 1024 * 1024
-LAG_NS = 2000
+LAG_NS = 3500
 
 score_scale = 1.0 / math.sqrt(192.0)
 very_low = -1e30

time: 80.9 us -> 79.8 us (0.986)
  blocking collectives: 76.2 us -> 75.1 us
    all_to_all x4, blocking collectives: 76.2 us -> 75.1 us  [exchanged(): return lax.all_to_all(value, axis, 0, 0, tiled=True)]
where the time goes in v10:
time: 79.8 us; the launch traced here: 79.5 us
  blocking collectives  75.1 us (94%)
  Pallas kernels  3.59 us (4%)
    all_to_all x4, blocking collectives, exchanged(): return lax.all_to_all(value, axis, 0, 0, tiled=True)  75.1 us

profile of v10, /device:TPU:1, one launch (start us, length us, event | category | flops | bytes accessed | tf_op | source)
XLA Modules:
  0.0 79.5 jit_solution(83129840304299617)
XLA Ops:
  0.0 0.0 copy-start
  0.7 0.8 %spread.1 = (bf16[32,56,128]{2,1,0:T(8,128)(2,1)S(1)}, f32[3,512]{1,0:T(4,128)S(1)}) custom-call(bf16[3,4,576]{2,1,0:T(4,128)(2,1)} %bitcast.8, s32[3,1,32]{2,1,0:T(1,128)} %bitcast.9, s32[1]{0:T(128)S(6)} %copy.7.position_ref), custom_call_target="tpu_custom_call" | custom-call | tf_op jit(solution)/shard_map/spread/pallas_call | solution.py:219
  1.6 25.8 %all_to_all.20.query_ref = bf16[32,56,128]{2,1,0:T(8,128)(2,1)S(1)} all-to-all(bf16[32,56,128]{2,1,0:T(8,128)(2,1)S(1)} %get-tuple-element.8), channel_id=1, replica_groups=mesh['req'=16,'seq'=32] {'seq'}, dimensions={0} | all-to-all | bytes 917504 | tf_op jit(solution)/shard_map/all_to_all | solution.py:198
  27.4 0.0 copy-done
  27.4 1.0 %attend.1 = bf16[32,13,4,128]{3,2,1,0:T(4,128)(2,1)S(1)} custom-call(f32[3,512]{1,0:T(4,128)S(1)} %get-tuple-element.7.usable_ref, bf16[32,56,128]{2,1,0:T(8,128)(2,1)S(1)} %all_to_all.20.query_ref, bf16[576,512]{1,0:T(8,128)(2,1)S(1)} %bitcast.6), custom_call_target="tpu_custom_call" | custom-call | tf_op jit(solution)/shard_map/attend/pallas_call | solution.py:240
  28.4 0.0 copy-start.1
  28.4 15.7 %all_to_all.21.parts_ref = bf16[32,13,4,128]{3,2,1,0:T(4,128)(2,1)S(1)} all-to-all(bf16[32,13,4,128]{3,2,1,0:T(4,128)(2,1)S(1)} %attend.1), channel_id=1, replica_groups=mesh['req'=16,'seq'=32] {'seq'}, dimensions={0} | all-to-all | bytes 851968 | tf_op jit(solution)/shard_map/all_to_all | solution.py:198
  44.1 0.0 copy-done.1
  44.1 0.0 copy-start.2
  44.1 0.6 merge.1
  44.7 21.1 %all_to_all.22.heads_ref = bf16[16,3,4,128]{3,2,1,0:T(4,128)(2,1)S(1)} all-to-all(bf16[16,3,4,128]{3,2,1,0:T(4,128)(2,1)S(1)} %merge.1), channel_id=1, replica_groups=mesh['req'=16,'seq'=32] {'req'}, dimensions={0} | all-to-all | bytes 98304 | tf_op jit(solution)/shard_map/all_to_all | solution.py:198
  65.8 0.0 copy-done.2
  65.8 0.5 project.1
  66.3 12.5 %all_to_all.23.parts_ref = bf16[32,7,96]{2,1,0:T(8,128)(2,1)S(1)} all-to-all(bf16[32,7,96]{2,1,0:T(8,128)(2,1)S(1)} %project.1), channel_id=1, replica_groups=mesh['req'=16,'seq'=32] {'seq'}, dimensions={0} | all-to-all | bytes 86016 | tf_op jit(solution)/shard_map/all_to_all | solution.py:198
  78.8 0.7 finish.1
Async XLA Ops:
  0.0 27.4 %copy-start = (bf16[1,512,576]{1,2,0:T(8,128)(2,1)S(1)}, bf16[1,512,576]{1,2,0:T(8,128)(2,1)}, u32[]{:S(2)}) copy-start(bf16[1,512,576]{1,2,0:T(8,128)(2,1)} %param.6) | copy-start | bytes 1769476
  28.4 15.7 %copy-start.1 = (bf16[4,512,128]{2,1,0:T(8,128)(2,1)S(1)}, bf16[4,512,128]{2,1,0:T(8,128)(2,1)}, u32[]{:S(2)}) copy-start(bf16[4,512,128]{2,1,0:T(8,128)(2,1)} %value_ref.1) | copy-start | bytes 1572868
  44.1 21.7 %copy-start.2 = (bf16[512,448]{0,1:T(8,128)(2,1)S(1)}, bf16[512,448]{0,1:T(8,128)(2,1)}, u32[]{:S(2)}) copy-start(bf16[512,448]{0,1:T(8,128)(2,1)} %param.11) | copy-start | bytes 1376260

commit v11 on v8

--- a/solution.py
+++ b/solution.py
@@ -5,6 +5,7 @@
 from jax import lax
 from jax.experimental import pallas as pl
 from jax.experimental.pallas import tpu as pltpu
+from jax.sharding import Mesh
 from jax.sharding import PartitionSpec as P
 
 LATENT = 512
@@ -14,6 +15,8 @@
 CHUNKS = LATENT // LANES
 GRANT = 12 * 1024 * 1024
 LAG_NS = 3000
+SEQ = ("z2", "z1", "z0", "x")
+ORDER = ("z0", "x", "z1", "z2")
 
 score_scale = 1.0 / math.sqrt(192.0)
 very_low = -1e30
@@ -55,7 +58,7 @@
         )
     cache_len = usable_ref.shape[1]
     blocks = cache_len // BLOCK
-    first = lax.axis_index("seq") * cache_len
+    first = lax.axis_index(SEQ) * cache_len
     column = lax.broadcasted_iota(jnp.int32, (blocks, cache_len), 1)
     mine = column // BLOCK == lax.broadcasted_iota(jnp.int32, (blocks, cache_len), 0)
     mine = mine & (first + column < position_ref[0])
@@ -211,7 +214,7 @@
 def body(latent_cache, queries, chosen, position, w_value, w_out):
     cache_len, key_width = latent_cache.shape[1:]
     _, steps, heads_dev, _ = queries.shape
-    shards = lax.axis_size("seq")
+    shards = lax.axis_size(SEQ)
     requests = lax.axis_size("req")
     heads = shards * heads_dev
 
@@ -236,7 +239,7 @@
         pltpu.with_memory_space_constraint(jnp.swapaxes(chosen, 0, 1), pltpu.HBM),
         position,
     )
-    query_all = exchanged(query_all, "seq")
+    query_all = exchanged(query_all, ORDER)
     parts = kernel(
         attend_kernel,
         (shards, steps * CHUNKS + 1, heads_dev, LANES),
@@ -248,7 +251,7 @@
             ((heads, LANES), bf16),
         ),
     )(usable, query_all, latent_cache[0].T)
-    parts = exchanged(parts, "seq")
+    parts = exchanged(parts, ORDER)
     head_out = kernel(merge_kernel, (requests, steps, heads_dev, w_value.shape[2]), "merge")(
         parts, w_value
     )
@@ -261,22 +264,24 @@
         "project",
         (((count * heads_dev, LANES), bf16), ((features, 2 * count), f32)),
     )(head_out, w_out.T)
-    mixed = exchanged(mixed, "seq")
+    mixed = exchanged(mixed, SEQ)
     return kernel(finish_kernel, (features // shards, count), "finish")(mixed)
 
 
 def solution(mesh):
+    requests, shards = mesh.devices.shape
+    fine = Mesh(mesh.devices.reshape(requests, 2, 2, 2, shards // 8), ("req", *SEQ))
     return jax.shard_map(
         body,
-        mesh=mesh,
+        mesh=fine,
         in_specs=(
-            P("req", "seq", None),
-            P("req", None, "seq", None),
+            P("req", SEQ, None),
+            P("req", None, SEQ, None),
             P("req", None, None),
             P("req"),
-            P("seq", None, None),
-            P("seq", "req"),
+            P(SEQ, None, None),
+            P(SEQ, "req"),
         ),
-        out_specs=P(("req", "seq"), None),
+        out_specs=P(("req", *SEQ), None),
         check_vma=False,
     )

time: 79.8 us -> 79.5 us (level)
  no operation moved by 1% of the time
where the time goes in v11:
time: 79.5 us; the launch traced here: 79.2 us
  blocking collectives  74.8 us (94%)
  Pallas kernels  3.58 us (5%)
    all_to_all x4, blocking collectives, exchanged(): return lax.all_to_all(value, axis, 0, 0, tiled=True)  74.8 us

profile of v11, /device:TPU:1, one launch (start us, length us, event | category | flops | bytes accessed | tf_op | source)
XLA Modules:
  0.0 79.2 jit_solution(13730297369783078217)
XLA Ops:
  0.0 0.0 copy-start
  0.7 0.8 %spread.1 = (bf16[32,56,128]{2,1,0:T(8,128)(2,1)S(1)}, f32[3,512]{1,0:T(4,128)S(1)}) custom-call(bf16[3,4,576]{2,1,0:T(4,128)(2,1)} %bitcast.8, s32[3,1,32]{2,1,0:T(1,128)} %bitcast.9, s32[1]{0:T(128)S(6)} %copy.7.position_ref), custom_call_target="tpu_custom_call" | custom-call | tf_op jit(solution)/shard_map/spread/pallas_call | solution.py:222
  1.6 25.3 %all_to_all.20.query_ref = bf16[32,56,128]{2,1,0:T(8,128)(2,1)S(1)} all-to-all(bf16[32,56,128]{2,1,0:T(8,128)(2,1)S(1)} %get-tuple-element.8), channel_id=1, replica_groups=mesh['req'=16,'z2'=2,'z1'=2,'z0'=2,'x'=4] {'z0','x','z1','z2'}, dimensions={0} | all-to-all | bytes 917504 | tf_op jit(solution)/shard_map/all_to_all | solution.py:201
  26.8 0.0 copy-done
  26.8 1.0 %attend.1 = bf16[32,13,4,128]{3,2,1,0:T(4,128)(2,1)S(1)} custom-call(f32[3,512]{1,0:T(4,128)S(1)} %get-tuple-element.7.usable_ref, bf16[32,56,128]{2,1,0:T(8,128)(2,1)S(1)} %all_to_all.20.query_ref, bf16[576,512]{1,0:T(8,128)(2,1)S(1)} %bitcast.6), custom_call_target="tpu_custom_call" | custom-call | tf_op jit(solution)/shard_map/attend/pallas_call | solution.py:243
  27.8 0.0 copy-start.1
  27.8 16.4 %all_to_all.21.parts_ref = bf16[32,13,4,128]{3,2,1,0:T(4,128)(2,1)S(1)} all-to-all(bf16[32,13,4,128]{3,2,1,0:T(4,128)(2,1)S(1)} %attend.1), channel_id=1, replica_groups=mesh['req'=16,'z2'=2,'z1'=2,'z0'=2,'x'=4] {'z0','x','z1','z2'}, dimensions={0} | all-to-all | bytes 851968 | tf_op jit(solution)/shard_map/all_to_all | solution.py:201
  44.2 0.0 copy-done.1
  44.2 0.0 copy-start.2
  44.2 0.6 merge.1
  44.8 20.3 %all_to_all.22.heads_ref = bf16[16,3,4,128]{3,2,1,0:T(4,128)(2,1)S(1)} all-to-all(bf16[16,3,4,128]{3,2,1,0:T(4,128)(2,1)S(1)} %merge.1), channel_id=1, replica_groups=mesh['req'=16,'z2'=2,'z1'=2,'z0'=2,'x'=4] {'req'}, dimensions={0} | all-to-all | bytes 98304 | tf_op jit(solution)/shard_map/all_to_all | solution.py:201
  65.1 0.0 copy-done.2
  65.1 0.5 project.1
  65.6 12.9 %all_to_all.23.parts_ref = bf16[32,7,96]{2,1,0:T(8,128)(2,1)S(1)} all-to-all(bf16[32,7,96]{2,1,0:T(8,128)(2,1)S(1)} %project.1), channel_id=1, replica_groups=mesh['req'=16,'z2'=2,'z1'=2,'z0'=2,'x'=4] {'z2','z1','z0','x'}, dimensions={0} | all-to-all | bytes 86016 | tf_op jit(solution)/shard_map/all_to_all | solution.py:201
  78.5 0.7 finish.1
Async XLA Ops:
  0.0 26.8 %copy-start = (bf16[1,512,576]{1,2,0:T(8,128)(2,1)S(1)}, bf16[1,512,576]{1,2,0:T(8,128)(2,1)}, u32[]{:S(2)}) copy-start(bf16[1,512,576]{1,2,0:T(8,128)(2,1)} %param.6) | copy-start | bytes 1769476
  27.8 16.4 %copy-start.1 = (bf16[4,512,128]{2,1,0:T(8,128)(2,1)S(1)}, bf16[4,512,128]{2,1,0:T(8,128)(2,1)}, u32[]{:S(2)}) copy-start(bf16[4,512,128]{2,1,0:T(8,128)(2,1)} %value_ref.1) | copy-start | bytes 1572868
  44.2 20.9 %copy-start.2 = (bf16[512,448]{0,1:T(8,128)(2,1)S(1)}, bf16[512,448]{0,1:T(8,128)(2,1)}, u32[]{:S(2)}) copy-start(bf16[512,448]{0,1:T(8,128)(2,1)} %param.11) | copy-start | bytes 1376260
